TPU v7x, 32 devices: a whole 2x2x4 slice. The times are simulated.
32 devices in a mesh: dp: 8 (over y, x, core), fsdp: 4 (over z).
Axes of the slice: x: 2, y: 2, z: 4, core: 2. Of those that a mesh axis runs over, the one named last changes fastest.
Arguments:
- tokens: bfloat16 [4096, 4096], P('dp'), may hold values from -6 to 6
- counts: int32 [8], P('dp'), may hold values from 256 to 512, as said below
- patch_index: int32 [4096], P('dp'), may hold values from 0 to 255
- clip_limit: float32 [], replicated, may hold values from 1024 to 8192
- norm_gain: float32 [4, 4096], replicated, may hold values from 0.25 to 1.75
- params: float32 [4, 4096, 4096], P(None, 'dp', 'fsdp'), may hold values from -0.09375 to 0.09375
- moments: float32 [4, 4096, 4096], P(None, 'dp', 'fsdp'), may hold values from -0.3 to 0.3
- seconds: float32 [4, 4096, 4096], P(None, 'dp', 'fsdp'), may hold values from 0.05 to 1
- gradients: float32 [4, 4096, 4096], P(None, 'dp', 'fsdp'), may hold values from -48 to 48
Outputs:
- params_new: float32 [4, 4096, 4096], P(None, 'dp', 'fsdp')
- moments_new: float32 [4, 4096, 4096], P(None, 'dp', 'fsdp')
- seconds_new: float32 [4, 4096, 4096], P(None, 'dp', 'fsdp')
- mixed: bfloat16 [4096, 4096], P('dp', 'fsdp')
Inputs may be any that keep to these rules, and one draw needn't show every extreme that they name: `counts`: at most 512, reached on some index of dp in every draw.
All inputs are finite; a program needn't handle non-finite values.
Results may differ from a plain program's by a relative error of at most 0.0095.
Values may be sent and summed in bfloat16 or wider, within the bound.
A program may use at most 192 MiB of HBM per device.

v0:
```python
import functools
import jax
import jax.numpy as jnp
from jax import lax
from jax.experimental import pallas as pl
from jax.experimental.pallas import tpu as pltpu
from jax.sharding import PartitionSpec as P

GRID = 16
STEP = 40

beta_one = 0.9
beta_two = 0.95
adam_eps = 1e-08
learning_rate = 0.0024
weight_decay = 0.05
norm_eps = 1e-06

MESH = pl.DeviceIdType.MESH
ANY = pl.BlockSpec(memory_space=pl.ANY)
VMEM = pl.BlockSpec(memory_space=pltpu.VMEM)
SMEM = pl.BlockSpec(memory_space=pltpu.SMEM)


def position_code(patch_index, width):
    quarter = width // 4
    freqs = 1.0 / 10000.0 ** (jnp.arange(quarter, dtype=jnp.float32) / quarter)
    across = (patch_index // GRID).astype(jnp.float32)[:, None] * freqs[None, :]
    downward = (patch_index % GRID).astype(jnp.float32)[:, None] * freqs[None, :]
    return jnp.concatenate(
        [jnp.sin(across), jnp.cos(across), jnp.sin(downward), jnp.cos(downward)], axis=1
    )


def adam_update(params, moments, seconds, gradients, factor):
    clipped = gradients * factor
    moments_new = beta_one * moments + (1.0 - beta_one) * clipped
    seconds_new = beta_two * seconds + (1.0 - beta_two) * clipped * clipped
    direction = (
        moments_new
        / (1.0 - beta_one**STEP)
        / (jnp.sqrt(seconds_new / (1.0 - beta_two**STEP)) + adam_eps)
    )
    params_new = params - learning_rate * (direction + weight_decay * params)
    return (params_new, moments_new, seconds_new)


def total_kernel(sizes, x_ref, o_ref, *scratch):
    names = ("dp", "fsdp")
    mid, got, send, recv = scratch[0], scratch[1:3], scratch[3:5], scratch[5:7]
    place = [lax.axis_index(name) for name in names]
    barrier = pltpu.get_barrier_semaphore()
    for axis in range(2):
        for step in range(1, sizes[axis]):
            pl.semaphore_signal(
                barrier,
                inc=1,
                device_id={names[axis]: lax.rem(place[axis] + step, sizes[axis])},
                device_id_type=MESH,
            )
    pl.semaphore_wait(barrier, sizes[0] + sizes[1] - 2)
    for axis in range(2):
        source = x_ref if axis == 0 else mid
        copies = []
        for step in range(1, sizes[axis]):
            copy = pltpu.make_async_remote_copy(
                src_ref=source,
                dst_ref=got[axis].at[place[axis]],
                send_sem=send[axis].at[step - 1],
                recv_sem=recv[axis].at[step - 1],
                device_id={names[axis]: lax.rem(place[axis] + step, sizes[axis])},
                device_id_type=MESH,
            )
            copy.start()
            copies.append(copy)
        got[axis][place[axis]] = source[...]
        for copy in copies:
            copy.wait()
        total = got[axis][0]
        for slot in range(1, sizes[axis]):
            total = total + got[axis][slot]
        if axis == 0:
            mid[...] = total
        else:
            o_ref[...] = total


def total_over_mesh(value, sizes):
    shape = (8, 128)
    total = pl.pallas_call(
        functools.partial(total_kernel, sizes),
        out_shape=jax.ShapeDtypeStruct(shape, jnp.float32),
        in_specs=[VMEM],
        out_specs=VMEM,
        scratch_shapes=[
            pltpu.VMEM(shape, jnp.float32),
            pltpu.VMEM((sizes[0],) + shape, jnp.float32),
            pltpu.VMEM((sizes[1],) + shape, jnp.float32),
        ]
        + [pltpu.SemaphoreType.DMA((max(size - 1, 1),)) for size in sizes] * 2,
        compiler_params=pltpu.CompilerParams(collective_id=0, has_side_effects=True),
        name="total",
    )(jnp.full(shape, value))
    return total[0, 0]


def layer_kernel(first, last, n, chunks, names, *refs):
    r = dict(zip(names, refs))
    place = lax.axis_index("fsdp")
    rows, width = r["stream"].shape
    cols = r["weights"].shape[1]
    part = rows // chunks
    half = cols // 2
    tile = min(256, half)
    tiles = cols // tile
    sub = 32

    def rows_of(c):
        return pl.ds(pl.multiple_of(c * part, part), part)

    def cols_of(owner):
        return pl.ds(pl.multiple_of(owner * cols, cols), cols)

    def take_stream(c):
        return pltpu.make_async_copy(
            r["stream"].at[rows_of(c)], r["s"].at[rows_of(c)], r["s_sem"].at[c]
        )

    def take_branch(c):
        return pltpu.make_async_copy(
            r["branch"].at[rows_of(c)], r["b"].at[rows_of(c)], r["b_sem"].at[c]
        )

    def take_weights(k):
        piece = pl.ds(pl.multiple_of(k * tile, tile), tile)
        return pltpu.make_async_copy(
            r["weights"].at[:, piece], r["w"].at[:, piece], r["w_sem"].at[k]
        )

    def put_stream(c):
        return pltpu.make_async_copy(
            r["s"].at[rows_of(c)], r["stream_out"].at[rows_of(c)], r["so_sem"].at[c]
        )

    def put_own(c):
        return pltpu.make_async_copy(
            r["own"].at[rows_of(c)],
            r["branch_out"].at[rows_of(c), cols_of(place)],
            r["own_sem"].at[c],
        )

    def pass_on(way, hop, c, side):
        owner = place - hop if way == 0 else place + hop
        target = r["branch_out"].at[
            rows_of(c), pl.ds(pl.multiple_of(owner * cols + side * half, half), half)
        ]
        source = r["own"].at[rows_of(c), pl.ds(side * half, half)] if hop == 0 else target
        peer = lax.rem(place + 1, n) if way == 0 else lax.rem(place + n - 1, n)
        return pltpu.make_async_remote_copy(
            src_ref=source,
            dst_ref=target,
            send_sem=r["send"].at[way, hop, 2 * c + side],
            recv_sem=r["recv"].at[way, hop, 2 * c + side],
            device_id={"fsdp": peer},
            device_id_type=MESH,
        )

    def has_sent(way, hop):
        if way == 0:
            return jnp.logical_and(place < n - 1, place >= hop)
        return jnp.logical_and(place > 0, place + hop < n)

    def has_got(way, hop):
        return place >= hop + 1 if way == 0 else place + hop + 1 < n

    def take_rows(c):
        take_stream(c).start()
        if not first:
            take_branch(c).start()

    take_rows(0)
    for k in range(tiles):
        take_weights(k).start()

    if not last:
        barrier = pltpu.get_barrier_semaphore()
        for step in (1, n - 1):
            pl.semaphore_signal(
                barrier, inc=1, device_id={"fsdp": lax.rem(place + step, n)}, device_id_type=MESH
            )
        pl.semaphore_wait(barrier, 2)

    def chunk_body(c, carry):
        take_stream(c).wait()
        if not first:
            take_branch(c).wait()

        def norm_body(k, carry):
            at = pl.ds(pl.multiple_of(c * part + k * sub, sub), sub)
            x = r["s"][at]
            if not first:
                x = x + r["b"][at].astype(jnp.float32)
                r["s"][at] = x
            centre = jnp.sum(x, axis=1, keepdims=True) * (1.0 / width)
            shifted = x - centre
            spread = jnp.sum(shifted * shifted, axis=1, keepdims=True) * (1.0 / width)
            normed = shifted * lax.rsqrt(spread + norm_eps) * r["gain"][...]
            r["x"][pl.ds(pl.multiple_of(k * sub, sub), sub)] = normed.astype(jnp.bfloat16)
            return carry

        lax.fori_loop(0, part // sub, norm_body, 0)
        if "stream_out" in r:
            put_stream(c).start()

        def dot_body(t, carry):
            @pl.when(c == 0)
            def _():
                take_weights(t).wait()

                @pl.when(t == tiles // 2 - 1)
                def _():
                    for later in range(1, chunks):
                        take_rows(later)

            at = pl.ds(pl.multiple_of(t * tile, tile), tile)
            out = jnp.dot(
                r["x"][...], r["w"][:, at], preferred_element_type=jnp.float32
            ).astype(jnp.bfloat16)
            if last:
                mine = pl.ds(pl.multiple_of(place * cols + t * tile, tile), tile)
                slot = c * part + lax.broadcasted_iota(jnp.int32, (part, tile), 0)
                total = r["s"][rows_of(c), mine] + out.astype(jnp.float32)
                total = jnp.where(slot < r["counts"][0], total, 0.0)
                r["mixed"][rows_of(c), at] = total.astype(jnp.bfloat16)
            else:
                r["own"][rows_of(c), at] = out
            return carry

        for side in range(2):
            lax.fori_loop(side * tiles // 2, (side + 1) * tiles // 2, dot_body, 0)
            if not last:
                for way in range(2):

                    @pl.when(has_sent(way, 0))
                    def _():
                        pass_on(way, 0, c, side).start()

        if not last:
            put_own(c).start()
        return carry

    lax.fori_loop(0, chunks, chunk_body, 0)
    if last:
        return

    for hop in range(n - 1):

        def forward_body(c, carry):
            for side in range(2):
                for way in range(2):

                    @pl.when(has_got(way, hop))
                    def _():
                        pass_on(way, hop, c, side).wait_recv()

                    if hop + 1 < n - 1:

                        @pl.when(has_sent(way, hop + 1))
                        def _():
                            pass_on(way, hop + 1, c, side).start()

            return carry

        lax.fori_loop(0, chunks, forward_body, 0)

    def finish_body(c, carry):
        put_own(c).wait()
        if "stream_out" in r:
            put_stream(c).wait()
        for hop in range(n - 1):
            for way in range(2):

                @pl.when(has_sent(way, hop))
                def _():
                    for side in range(2):
                        pass_on(way, hop, c, side).wait_send()

        return carry

    lax.fori_loop(0, chunks, finish_body, 0)


def run_layer(current, layers, n, stream, branch, gain, weights, counts):
    first, last = current == 0, current + 1 == layers
    rows, width = stream.shape
    cols = weights.shape[1]
    chunks = 4
    part = rows // chunks
    dma = pltpu.SemaphoreType.DMA
    names, args, specs = ["stream"], [stream], [ANY]
    if not first:
        names, args, specs = names + ["branch"], args + [branch], specs + [ANY]
    names, args, specs = (
        names + ["gain", "weights"],
        args + [gain, weights],
        specs + [VMEM, ANY],
    )
    if last:
        names, args, specs = names + ["counts"], args + [counts], specs + [SMEM]
        out_names, out_shape, out_specs = (
            ["mixed"],
            [jax.ShapeDtypeStruct((rows, cols), jnp.bfloat16)],
            [VMEM],
        )
    else:
        out_names, out_shape = ["branch_out"], [jax.ShapeDtypeStruct((rows, width), jnp.bfloat16)]
        if not first:
            out_names = out_names + ["stream_out"]
            out_shape = out_shape + [jax.ShapeDtypeStruct((rows, width), jnp.float32)]
        out_specs = [ANY] * len(out_names)
    scratch = {
        "s": pltpu.VMEM((rows, width), jnp.float32),
        "w": pltpu.VMEM(weights.shape, jnp.bfloat16),
        "x": pltpu.VMEM((part, width), jnp.bfloat16),
        "s_sem": dma((chunks,)),
        "w_sem": dma((cols // min(256, cols // 2),)),
    }
    if not first:
        scratch["b"] = pltpu.VMEM((rows, width), jnp.bfloat16)
        scratch["b_sem"] = dma((chunks,))
    if not last:
        scratch["own"] = pltpu.VMEM((rows, cols), jnp.bfloat16)
        scratch["own_sem"] = dma((chunks,))
        scratch["send"] = dma((2, n - 1, 2 * chunks))
        scratch["recv"] = dma((2, n - 1, 2 * chunks))
        if not first:
            scratch["so_sem"] = dma((chunks,))
    size = rows * cols
    out = pl.pallas_call(
        functools.partial(
            layer_kernel, first, last, n, chunks, names + out_names + list(scratch)
        ),
        out_shape=out_shape,
        in_specs=specs,
        out_specs=out_specs,
        scratch_shapes=list(scratch.values()),
        compiler_params=pltpu.CompilerParams(
            collective_id=None if last else 1 + current,
            has_side_effects=not last,
            vmem_limit_bytes=63 * 2**20,
        ),
        cost_estimate=pl.CostEstimate(
            flops=2 * size * width,
            bytes_accessed=(40 if last else 240) * size,
            transcendentals=0,
        ),
        name="last_layer" if last else "layer_%d" % current,
    )(*args)
    if last:
        return None, None, out[0]
    return (stream if first else out[1]), out[0], None


def per_device(
    sizes,
    tokens,
    counts,
    patch_index,
    clip_limit,
    norm_gain,
    params,
    moments,
    seconds,
    gradients,
):
    layers = params.shape[0]
    squares = total_over_mesh(jnp.sum(gradients * gradients), sizes)
    factor = jnp.minimum(1.0, clip_limit / (jnp.sqrt(squares) + 1e-06))
    head = adam_update(params[0], moments[0], seconds[0], gradients[0], factor)[0]
    head = head.astype(jnp.bfloat16)
    later_factor, head, patch_index = lax.optimization_barrier((factor, head, patch_index))
    params_new, moments_new, seconds_new = adam_update(
        params, moments, seconds, gradients, later_factor
    )
    weights = lax.all_gather(head, "dp", axis=0, tiled=True)
    tok_rows = tokens.shape[0]
    valid = lax.broadcasted_iota(jnp.int32, (tok_rows, 1), 0) < counts[0]
    stream = jnp.where(
        valid, tokens.astype(jnp.float32) + position_code(patch_index, tokens.shape[1]), 0.0
    )
    branch = mixed = following = None
    for current in range(layers):
        if current + 1 < layers:
            piece = params_new[current + 1].astype(jnp.bfloat16)
            ready = stream if current == 0 else branch
            piece, weights, ready = lax.optimization_barrier((piece, weights, ready))
            stream, branch = (ready, None) if current == 0 else (stream, ready)
            following = lax.all_gather(piece, "dp", axis=0, tiled=True)
        stream, branch, mixed = run_layer(
            current,
            layers,
            sizes[1],
            stream,
            branch,
            norm_gain[current][None],
            weights,
            counts,
        )
        weights = following
    return (params_new, moments_new, seconds_new, mixed)


def solution(mesh):
    sizes = (mesh.shape["dp"], mesh.shape["fsdp"])
    weight = P(None, "dp", "fsdp")
    return jax.shard_map(
        functools.partial(per_device, sizes),
        mesh=mesh,
        in_specs=(P("dp", None), P("dp"), P("dp"), P(), P(), weight, weight, weight, weight),
        out_specs=(weight, weight, weight, P("dp", "fsdp")),
        check_vma=False,
    )
```

profile of v0, /device:TPU:0, one launch (start us, length us, event | category | flops | bytes accessed | tf_op | source)
XLA Modules:
  0.0 345.9 jit_solution(1020022632810429146)
XLA Ops:
  7.2 0.0 all-gather.5.cloned.1.call-start
  7.9 0.0 copy-start.2
  7.9 6.1 %multiply_reduce_fusion = f32[]{:T(128)} fusion(f32[4,512,1024]{2,1,0:T(8,128)} %param.17), kind=kLoop, calls=%fused_computation.6 | loop fusion | flops 4194303 | bytes 8388612 | tf_op jit(solution)/shard_map/reduce_sum | solution.py:377
  14.0 1.2 broadcast_in_dim.19.x_ref
  15.3 12.8 %total.1 = f32[8,128]{1,0:T(8,128)} custom-call(f32[8,128]{1,0:T(8,128)} %broadcast_in_dim.19.x_ref), custom_call_target="tpu_custom_call" | custom-call | tf_op jit(solution)/shard_map/total/pallas_call | solution.py:90
  28.1 1.2 slice.39
  30.0 6.2 %fusion.10 = bf16[512,1024]{1,0:T(8,128)(2,1)} fusion(f32[4,512,1024]{2,1,0:T(8,128)} %param.16, f32[4,512,1024]{2,1,0:T(8,128)} %param.17, f32[4,512,1024]{2,1,0:T(8,128)} %param.15, f32[4,512,1024]{2,1,0:T(8,128)} %param.14, f32[]{:T(128)S(6)} %min.3), kind=kLoop, calls=%fused_computation.23 | loop fusion | flops 8912896 | bytes 9437188 | tf_op jit(solution)/shard_map/convert_element_type | solution.py:380
  36.2 0.0 all-gather.5.cloned.1.call-update
  36.2 0.2 all-gather.7.cloned.1.call-start
  37.1 0.0 copy-done.2
  37.2 21.4 %fusion.14 = (bf16[4,512,1024]{2,1,0:T(8,128)(2,1)}, f32[4,512,1024]{2,1,0:T(8,128)}, f32[4,512,1024]{2,1,0:T(8,128)}, f32[4,512,1024]{2,1,0:T(8,128)}) fusion(f32[4,512,1024]{2,1,0:T(8,128)} %param.14, f32[4,512,1024]{2,1,0:T(8,128)} %param.17, f32[]{:T(128)S(6)} %min.3, f32[4,512,1024]{2,1,0:T(8,128)} %param.15, f32[4,512,1024]{2,1,0:T(8,128)} %param.16), kind=kLoop, calls=%fused_computation.39 | loop fusion | flops 35651584 | bytes 62914564 | tf_op jit(solution)/shard_map/convert.2
  58.6 0.0 copy-start
  58.6 3.8 %slice_bitcast_fusion = (bf16[512,1024]{1,0:T(8,128)(2,1)}, bf16[512,1024]{1,0:T(8,128)(2,1)}, bf16[512,1024]{1,0:T(8,128)(2,1)}) fusion(bf16[4,512,1024]{2,1,0:T(8,128)(2,1)} %get-tuple-element.36), kind=kLoop, calls=%fused_computation.24 | loop fusion | bytes 6291456 | tf_op jit(solution)/shard_map/convert_element_type | solution.py:394
  62.5 14.7 %multiply_sine_fusion.1 = (f32[512,1024]{1,0:T(8,128)S(1)}, f32[512,1024]{1,0:T(8,128)S(1)}, f32[512,1024]{1,0:T(8,128)S(1)}, f32[512,1024]{1,0:T(8,128)S(1)}) fusion(f32[1024]{0:T(1024)S(1)} %negate_power_fusion, f32[512]{0:T(512)S(1)} %get-tuple-element.53, f32[512]{0:T(512)S(1)} %get-tuple-element.54), kind=kLoop, calls=%fused_computation.11 | loop fusion | flops 1048576 | bytes 8396800 | tf_op jit(solution)/shard_map/sin | solution.py:31
  77.2 0.0 copy-done
  77.2 0.0 copy-start.1
  77.2 4.1 %fusion.1.refs_0_ = f32[512,4096]{1,0:T(8,128)} fusion(f32[512,1024]{1,0:T(8,128)S(1)} %get-tuple-element.51, f32[512,1024]{1,0:T(8,128)S(1)} %get-tuple-element.52, f32[512,1024]{1,0:T(8,128)S(1)} %get-tuple-element.48, f32[512,1024]{1,0:T(8,128)S(1)} %get-tuple-element.47, bf16[512,4096]{1,0:T(8,128)(2,1)S(1)} %copy-done, pred[512]{0:T(512)(128)(4,1)S(1)} %iota_compare_fusion), kind=kLoop, calls=%fused_computation.3 | loop fusion | flops 12582912 | bytes 20972032 | tf_op jit(solution)/shard_map/jit(_where)/select_n | solution.py:388
  81.3 8.4 %all-gather.5.cloned.1.call-done.refs_2_ = bf16[4096,1024]{1,0:T(8,128)(2,1)} async-done(((bf16[512,1024]{1,0:T(8,128)(2,1)}), bf16[4096,1024]{1,0:T(8,128)(2,1)}) %all-gather.5.cloned.1.call-update) | async-done | bytes 8388624 | tf_op jit(solution)/shard_map/all_gather | solution.py:385
  89.8 0.0 all-gather.7.cloned.1.call-update
  89.8 0.3 all-gather.9.cloned.1.call-start
  90.0 0.0 copy-done.1
  90.1 0.7 fusion.16
  90.7 77.6 %layer_0.1.refs_1_ = bf16[512,4096]{1,0:T(8,128)(2,1)} custom-call(f32[512,4096]{1,0:T(8,128)} %fusion.1.refs_0_, f32[1,4096]{1,0:T(1,128)} %get-tuple-element.45.refs_1_, bf16[4096,1024]{1,0:T(8,128)(2,1)} %all-gather.5.cloned.1.call-done.refs_2_), custom_call_target="tpu_custom_call" | custom-call | flops 4294967296 | bytes 125829120 | tf_op jit(solution)/shard_map/layer_0/pallas_call | solution.py:339
  168.3 0.0 all-gather.7.cloned.1.call-done.refs_3_
  168.3 0.0 all-gather.9.cloned.1.call-update
  168.3 0.0 all-gather.11.cloned.1.call-start
  168.4 75.4 %layer_1.1 = (bf16[512,4096]{1,0:T(8,128)(2,1)}, f32[512,4096]{1,0:T(8,128)}) custom-call(f32[512,4096]{1,0:T(8,128)} %fusion.1.refs_0_, bf16[512,4096]{1,0:T(8,128)(2,1)} %layer_0.1.refs_1_, f32[1,4096]{1,0:T(1,128)} %get-tuple-element.44.refs_2_, bf16[4096,1024]{1,0:T(8,128)(2,1)} %all-gather.7.cloned.1.call-done.refs_3_), custom_call_target="tpu_custom_call" | custom-call | flops 4294967296 | bytes 125829120 | tf_op jit(solution)/shard_map/layer_1/pallas_call | solution.py:339
  243.8 0.0 all-gather.9.cloned.1.call-done.refs_3_
  243.9 0.0 all-gather.11.cloned.1.call-update
  243.9 74.9 %layer_2.1 = (bf16[512,4096]{1,0:T(8,128)(2,1)}, f32[512,4096]{1,0:T(8,128)}) custom-call(f32[512,4096]{1,0:T(8,128)} %get-tuple-element.28.refs_0_, bf16[512,4096]{1,0:T(8,128)(2,1)} %get-tuple-element.31.refs_1_, f32[1,4096]{1,0:T(1,128)} %get-tuple-element.46.refs_2_, bf16[4096,1024]{1,0:T(8,128)(2,1)} %all-gather.9.cloned.1.call-done.refs_3_), custom_call_target="tpu_custom_call" | custom-call | flops 4294967296 | bytes 125829120 | tf_op jit(solution)/shard_map/layer_2/pallas_call | solution.py:339
  318.8 0.0 all-gather.11.cloned.1.call-done.refs_3_
  318.8 20.5 %last_layer.1 = bf16[512,1024]{1,0:T(8,128)(2,1)} custom-call(f32[512,4096]{1,0:T(8,128)} %get-tuple-element.33.refs_0_, bf16[512,4096]{1,0:T(8,128)(2,1)} %get-tuple-element.34.refs_1_, f32[1,4096]{1,0:T(1,128)} %get-tuple-element.43.refs_2_, bf16[4096,1024]{1,0:T(8,128)(2,1)} %all-gather.11.cloned.1.call-done.refs_3_, s32[1]{0:T(128)} %copy.13.refs_4_), custom_call_target="tpu_custom_call" | custom-call | flops 4294967296 | bytes 20971520 | tf_op jit(solution)/shard_map/last_layer/pallas_call | solution.py:339
  (3 shorter events, 0.0 us)
Async XLA Ops:
  7.2 82.6 %all-gather.5.cloned.1.call-start = ((), (), s32[]{:S(2)}) async-start(), calls=%async_computation | async-start | bytes 9437184 | tf_op jit(solution)/shard_map/all_gather | solution.py:385
  7.9 29.3 %copy-start.2 = (s32[512]{0:T(512)S(1)}, s32[512]{0:T(512)}, u32[]{:S(2)}) copy-start(s32[512]{0:T(512)} %param.11) | copy-start | bytes 6148
  36.2 132.1 %all-gather.7.cloned.1.call-start = ((), (), s32[]{:S(2)}) async-start(), calls=%async_computation.1 | async-start | bytes 9437184 | tf_op jit(solution)/shard_map/all_gather | solution.py:398
  58.6 18.6 %copy-start = (bf16[512,4096]{1,0:T(8,128)(2,1)S(1)}, bf16[512,4096]{1,0:T(8,128)(2,1)}, u32[]{:S(2)}) copy-start(bf16[512,4096]{1,0:T(8,128)(2,1)} %param.9) | copy-start | bytes 12582916
  77.2 12.9 %copy-start.1 = (f32[4,4096]{1,0:T(4,128)S(1)}, f32[4,4096]{1,0:T(4,128)}, u32[]{:S(2)}) copy-start(f32[4,4096]{1,0:T(4,128)} %param.13) | copy-start | bytes 196612
  89.8 154.1 %all-gather.9.cloned.1.call-start = ((), (), s32[]{:S(2)}) async-start(), calls=%async_computation.2 | async-start | bytes 9437184 | tf_op jit(solution)/shard_map/all_gather | solution.py:398
  168.3 150.4 %all-gather.11.cloned.1.call-start = ((), (), s32[]{:S(2)}) async-start(), calls=%async_computation.3 | async-start | bytes 9437184 | tf_op jit(solution)/shard_map/all_gather | solution.py:398
Sparse Core Ops, SparseCore 0:
  36.4 53.3 all-gather.4
  91.6 54.2 all-gather.6
  168.4 53.3 all-gather.8
  244.0 53.2 all-gather.10
where the time goes:
time: 346 us
  Pallas kernels  261 us (75%)
  other arithmetic  52.6 us (15%)
  between operations  15.9 us (5%)
  waiting for transfers between devices  8.56 us (2%)
  local copies, waits for them, and re-layouts  6.94 us (2%)
    pallas_call x4, Pallas kernels, run_layer(): pl.pallas_call(functools.partial(layer_kernel, first, last, n, chunks, na...  248 us
    another operation x1, other arithmetic  21.4 us
    sin x1, other arithmetic, position_code(): jnp.sin(across)  14.7 us
    pallas_call x1, Pallas kernels, total_over_mesh(): pl.pallas_call(functools.partial(total_kernel, sizes), out_shape=jax.Shap...  12.8 us
    all_gather x1, waiting for transfers between devices, per_device(): weights = lax.all_gather(head, 'dp', axis=0, tiled=True)  8.43 us
  transfers between devices with their start and end apart: 4, of which 1 were waited for; matrix products, arithmetic and copies ran while one was open for 13% of the time, Pallas kernels for 66%

commit v1 on v0

v1 whole, which is shorter than its diff:
```python
import functools
import jax
import jax.numpy as jnp
from jax import lax
from jax.experimental import pallas as pl
from jax.experimental.pallas import tpu as pltpu
from jax.sharding import PartitionSpec as P

GRID = 16
STEP = 40

beta_one = 0.9
beta_two = 0.95
adam_eps = 1e-08
learning_rate = 0.0024
weight_decay = 0.05
norm_eps = 1e-06

MESH = pl.DeviceIdType.MESH
ANY = pl.BlockSpec(memory_space=pl.ANY)
VMEM = pl.BlockSpec(memory_space=pltpu.VMEM)
SMEM = pl.BlockSpec(memory_space=pltpu.SMEM)


def adam_update(params, moments, seconds, gradients, factor):
    clipped = gradients * factor
    moments_new = beta_one * moments + (1.0 - beta_one) * clipped
    seconds_new = beta_two * seconds + (1.0 - beta_two) * clipped * clipped
    direction = (moments_new * (1.0 / (1.0 - beta_one**STEP))) / (
        jnp.sqrt(seconds_new * (1.0 / (1.0 - beta_two**STEP))) + adam_eps
    )
    params_new = params - learning_rate * (direction + weight_decay * params)
    return (params_new, moments_new, seconds_new)


def total_kernel(sizes, chunks, clip_ref, g_ref, p_ref, m_ref, s_ref, factor_ref, head_ref, *scratch):
    g, p, m, s, mine, mid, got0, got1 = scratch[:8]
    g_sem, a_sem, send0, send1, recv0, recv1 = scratch[8:]
    names, got, send, recv = ("dp", "fsdp"), (got0, got1), (send0, send1), (recv0, recv1)
    place = [lax.axis_index(name) for name in names]
    layers, rows, cols = g.shape
    part = rows // chunks

    def take_gradients(l, c):
        at = pl.ds(pl.multiple_of(c * part, part), part)
        return pltpu.make_async_copy(g_ref.at[l, at], g.at[l, at], g_sem.at[l, c])

    def start_layer(l, carry):
        lax.fori_loop(0, chunks, lambda c, x: (take_gradients(l, c).start(), x)[1], 0)
        return carry

    lax.fori_loop(0, layers, start_layer, 0)
    heads = [
        pltpu.make_async_copy(ref.at[0], to, a_sem.at[i])
        for i, (ref, to) in enumerate(((p_ref, p), (m_ref, m), (s_ref, s)))
    ]
    for copy in heads:
        copy.start()
    barrier = pltpu.get_barrier_semaphore()
    for axis in range(2):
        for step in range(1, sizes[axis]):
            pl.semaphore_signal(
                barrier,
                inc=1,
                device_id={names[axis]: lax.rem(place[axis] + step, sizes[axis])},
                device_id_type=MESH,
            )

    def add_layer(l, total):
        def add_chunk(c, total):
            take_gradients(l, c).wait()

            def add_rows(k, total):
                x = g[l, pl.ds(pl.multiple_of(c * part + k * 32, 32), 32)]
                x = x * x
                sums = [x[8 * i : 8 * i + 8] for i in range(4)]
                y = (sums[0] + sums[1]) + (sums[2] + sums[3])
                return total + y

            return lax.fori_loop(0, part // 32, add_rows, total)

        return lax.fori_loop(0, chunks, add_chunk, total)

    wide = lax.fori_loop(0, layers, add_layer, jnp.zeros((8, cols), jnp.float32))
    total = wide[:, 0:128]
    for k in range(1, cols // 128):
        total = total + wide[:, 128 * k : 128 * k + 128]
    mine[...] = total

    pl.semaphore_wait(barrier, sizes[0] + sizes[1] - 2)
    for axis in range(2):
        source = mine if axis == 0 else mid
        copies = []
        for step in range(1, sizes[axis]):
            copy = pltpu.make_async_remote_copy(
                src_ref=source,
                dst_ref=got[axis].at[place[axis]],
                send_sem=send[axis].at[step - 1],
                recv_sem=recv[axis].at[step - 1],
                device_id={names[axis]: lax.rem(place[axis] + step, sizes[axis])},
                device_id_type=MESH,
            )
            copy.start()
            copies.append(copy)
        got[axis][place[axis]] = source[...]
        for copy in copies:
            copy.wait()
        total = got[axis][0]
        for slot in range(1, sizes[axis]):
            total = total + got[axis][slot]
        if axis == 0:
            mid[...] = total
    squares = jnp.sum(jnp.sum(total, axis=1, keepdims=True), axis=0, keepdims=True)
    factor = jnp.minimum(1.0, clip_ref[0] / (jnp.sqrt(squares) + 1e-06))
    factor_ref[...] = jnp.broadcast_to(factor, factor_ref.shape)
    for copy in heads:
        copy.wait()

    def update(k, carry):
        at = pl.ds(pl.multiple_of(k * 16, 16), 16)
        head_ref[at] = adam_update(p[at], m[at], s[at], g[0, at], factor)[0].astype(jnp.bfloat16)
        return carry

    lax.fori_loop(0, rows // 16, update, 0)


def total_over_mesh(sizes, clip_limit, gradients, params, moments, seconds):
    layers, rows, cols = gradients.shape
    shape, f32, dma = (8, 128), jnp.float32, pltpu.SemaphoreType.DMA
    chunks = 2
    return pl.pallas_call(
        functools.partial(total_kernel, sizes, chunks),
        out_shape=[
            jax.ShapeDtypeStruct((8, 128), f32),
            jax.ShapeDtypeStruct((rows, cols), jnp.bfloat16),
        ],
        in_specs=[SMEM, ANY, ANY, ANY, ANY],
        out_specs=[VMEM, VMEM],
        scratch_shapes=[pltpu.VMEM((layers, rows, cols), f32)]
        + [pltpu.VMEM((rows, cols), f32)] * 3
        + [pltpu.VMEM(shape, f32)] * 2
        + [pltpu.VMEM((size,) + shape, f32) for size in sizes]
        + [dma((layers, chunks)), dma((3,))]
        + [dma((max(size - 1, 1),)) for size in sizes] * 2,
        compiler_params=pltpu.CompilerParams(
            collective_id=0, has_side_effects=True, vmem_limit_bytes=63 * 2**20
        ),
        name="total",
    )(clip_limit[None], gradients, params, moments, seconds)


def adam_kernel(f_ref, p_ref, m_ref, s_ref, g_ref, po_ref, mo_ref, so_ref, w_ref):
    factor = f_ref[0:1, 0:1]

    def update(k, carry):
        at = pl.ds(pl.multiple_of(k * 16, 16), 16)
        new = adam_update(p_ref[0, at], m_ref[0, at], s_ref[0, at], g_ref[0, at], factor)
        po_ref[0, at], mo_ref[0, at], so_ref[0, at] = new
        w_ref[0, at] = new[0].astype(jnp.bfloat16)
        return carry

    lax.fori_loop(0, p_ref.shape[1] // 16, update, 0)


def adam_all(factor, params, moments, seconds, gradients):
    layers, rows, cols = params.shape
    part = 128
    block = pl.BlockSpec((1, part, cols), lambda l, c: (l, c, 0))
    f32 = jax.ShapeDtypeStruct(params.shape, jnp.float32)
    return pl.pallas_call(
        adam_kernel,
        grid=(layers, rows // part),
        out_shape=[f32, f32, f32, jax.ShapeDtypeStruct(params.shape, jnp.bfloat16)],
        in_specs=[pl.BlockSpec((8, 128), lambda l, c: (0, 0))] + [block] * 4,
        out_specs=[block] * 4,
        compiler_params=pltpu.CompilerParams(vmem_limit_bytes=63 * 2**20),
        cost_estimate=pl.CostEstimate(
            flops=20 * params.size, bytes_accessed=30 * params.size, transcendentals=0
        ),
        name="adam",
    )(factor, params, moments, seconds, gradients)


def layers_kernel(n_dp, n, chunks, names, *refs):
    r = dict(zip(names, refs))
    layers, rows, cols = r["own"].shape
    tok, width = r["stream"].shape
    part = tok // chunks
    tile = min(256, cols)
    tiles = cols // tile
    sub_rows = rows // 2
    ring = n_dp // 2
    half = ring // 2
    hops = n - 1
    dp, place = lax.axis_index("dp"), lax.axis_index("fsdp")
    chip, core = dp // 2, lax.rem(dp, 2)
    count = r["counts"][0]

    def turn(i):
        if ring != 4:
            return i
        return (i // 2) * 2 + lax.rem(i + i // 2, 2)

    pos = turn(chip)

    def dp_of(position, which):
        return turn(lax.rem(position + 2 * ring, ring)) * 2 + which

    def w_rows(position, which, sub):
        at = dp_of(position, which) * rows + sub * sub_rows
        return pl.ds(pl.multiple_of(at, sub_rows), sub_rows)

    def rows_of(c):
        return pl.ds(pl.multiple_of(c * part, part), part)

    def cols_of(owner):
        return pl.ds(pl.multiple_of(owner * cols, cols), cols)

    def take_own(l):
        return pltpu.make_async_copy(
            r["own"].at[l],
            r["w"].at[l, pl.ds(pl.multiple_of(dp * rows, rows), rows)],
            r["own_sem"].at[l],
        )

    def ring_copy(l, way, hop, sub):
        owner = pos - hop if way == 0 else pos + hop
        at = w_rows(owner, core, sub)
        return pltpu.make_async_remote_copy(
            src_ref=r["w"].at[l, at],
            dst_ref=r["w"].at[l, at],
            send_sem=r["ring_send"].at[l, way, hop, sub],
            recv_sem=r["ring_recv"].at[l, way, hop, sub],
            device_id={"dp": dp_of(pos + 1 if way == 0 else pos - 1, core)},
            device_id_type=MESH,
        )

    def mate_copy(l, owner, slot, sub):
        at = w_rows(owner, core, sub)
        return pltpu.make_async_remote_copy(
            src_ref=r["w"].at[l, at],
            dst_ref=r["w"].at[l, at],
            send_sem=r["mate_send"].at[l, slot, sub],
            recv_sem=r["mate_recv"].at[l, slot, sub],
            device_id={"dp": chip * 2 + 1 - core},
            device_id_type=MESH,
        )

    def came(way, hop):
        return pos - 1 - hop if way == 0 else pos + 1 + hop

    def all_mates():
        out = [(pos, 0, 0), (pos, 0, 1)]
        for hop in range(half):
            for way in range(2):
                for sub in range(2):
                    if hop < half - 1 or sub == way:
                        out.append((came(way, hop), 1 + 2 * hop + way, sub))
        return out

    def all_rings():
        out = []
        for hop in range(half):
            for way in range(2):
                for sub in range(2):
                    if hop < half - 1 or sub == way:
                        out.append((way, hop, sub))
        return out

    ring_order = ((0, 0), (1, 1), (0, 1), (1, 0))

    def gather_start(l):
        take_own(l).wait()
        for way, sub in ring_order:
            if half > 1 or sub == way:
                ring_copy(l, way, 0, sub).start()
        for sub in range(2):
            mate_copy(l, pos, 0, sub).start()

    def gather_mid(l):
        for hop in range(half - 1):
            for way, sub in ring_order:
                ring_copy(l, way, hop, sub).wait_recv()
                if hop + 1 < half - 1 or sub == way:
                    ring_copy(l, way, hop + 1, sub).start()
                mate_copy(l, came(way, hop), 1 + 2 * hop + way, sub).start()

    def gather_end(l):
        hop = half - 1
        for way in range(2):
            ring_copy(l, way, hop, way).wait_recv()
            mate_copy(l, came(way, hop), 1 + 2 * hop + way, way).start()
        for owner, slot, sub in all_mates():
            mate_copy(l, owner, slot, sub).wait_recv()

    def pass_on(l, way, hop, c):
        owner = place - hop if way == 0 else place + hop
        peer = lax.rem(place + 1, n) if way == 0 else lax.rem(place + n - 1, n)
        target = r["b"].at[l, rows_of(c), cols_of(owner)]
        return pltpu.make_async_remote_copy(
            src_ref=target,
            dst_ref=target,
            send_sem=r["send"].at[l, way, hop, c],
            recv_sem=r["recv"].at[l, way, hop, c],
            device_id={"fsdp": peer},
            device_id_type=MESH,
        )

    def has_sent(way, hop):
        if way == 0:
            return jnp.logical_and(place < n - 1, place >= hop)
        return jnp.logical_and(place > 0, place + hop < n)

    def has_got(way, hop):
        return place >= hop + 1 if way == 0 else place + hop + 1 < n

    take_tokens = pltpu.make_async_copy(r["tokens"], r["b"].at[layers - 2], r["tok_sem"].at[0])
    take_tokens.start()
    for l in range(layers):
        take_own(l).start()

    barrier = pltpu.get_barrier_semaphore()
    peers = [{"fsdp": lax.rem(place + 1, n)}, {"fsdp": lax.rem(place + n - 1, n)}]
    peers += [{"dp": dp_of(pos + 1, core)}, {"dp": dp_of(pos - 1, core)}]
    peers += [{"dp": chip * 2 + 1 - core}]
    for peer in peers:
        pl.semaphore_signal(barrier, inc=1, device_id=peer, device_id_type=MESH)
    pl.semaphore_wait(barrier, len(peers))

    gather_start(0)
    take_tokens.wait()

    def init_body(t, carry):
        at = pl.ds(pl.multiple_of(t * tile, tile), tile)
        code = jnp.dot(r["hot"][...], r["table"][:, at], preferred_element_type=jnp.float32)
        slot = lax.broadcasted_iota(jnp.int32, code.shape, 0)
        value = r["b"][layers - 2, :, at].astype(jnp.float32) + code
        r["stream"][:, at] = jnp.where(slot < count, value, 0.0)
        return carry

    lax.fori_loop(0, width // tile, init_body, 0)
    gather_mid(0)
    gather_end(0)

    sub = 32

    def norm_chunk(l, c):
        def norm_body(k, carry):
            at = pl.ds(pl.multiple_of(c * part + k * sub, sub), sub)
            x = r["stream"][at]
            centre = jnp.sum(x, axis=1, keepdims=True) * (1.0 / width)
            shifted = x - centre
            spread = jnp.sum(shifted * shifted, axis=1, keepdims=True) * (1.0 / width)
            normed = shifted * lax.rsqrt(spread + norm_eps) * r["gain"][l]
            r["x"][pl.ds(pl.multiple_of(k * sub, sub), sub)] = normed.astype(jnp.bfloat16)
            return carry

        lax.fori_loop(0, part // sub, norm_body, 0)

    def add_chunk(l, c):
        for way in range(2):

            @pl.when(has_got(way, hops - 1))
            def _():
                pass_on(l - 1, way, hops - 1, c).wait_recv()

        def add_body(k, carry):
            at = pl.ds(pl.multiple_of(c * part + k * sub, sub), sub)
            r["stream"][at] = r["stream"][at] + r["b"][l - 1, at].astype(jnp.float32)
            return carry

        lax.fori_loop(0, part // sub, add_body, 0)

    def layer_body(l, carry):
        gather_start(l + 1)

        def chunk_body(c, carry):
            @pl.when(l > 0)
            def _():
                add_chunk(l, c)

            norm_chunk(l, c)

            def dot_body(t, carry):
                at = pl.ds(pl.multiple_of(t * tile, tile), tile)
                out = jnp.dot(r["x"][...], r["w"][l, :, at], preferred_element_type=jnp.float32)
                mine = pl.ds(pl.multiple_of(place * cols + t * tile, tile), tile)
                r["b"][l, rows_of(c), mine] = out.astype(jnp.bfloat16)
                return carry

            lax.fori_loop(0, tiles, dot_body, 0)
            for way in range(2):

                @pl.when(has_sent(way, 0))
                def _():
                    pass_on(l, way, 0, c).start()

            return carry

        lax.fori_loop(0, chunks, chunk_body, 0)
        for hop in range(hops - 1):

            def forward_body(c, carry):
                for way in range(2):

                    @pl.when(has_got(way, hop))
                    def _():
                        pass_on(l, way, hop, c).wait_recv()

                    @pl.when(has_sent(way, hop + 1))
                    def _():
                        pass_on(l, way, hop + 1, c).start()

                return carry

            lax.fori_loop(0, chunks, forward_body, 0)
            if hop == 0:
                gather_mid(l + 1)
        gather_end(l + 1)
        return carry

    lax.fori_loop(0, layers - 1, layer_body, 0)

    last = layers - 1

    def last_body(c, carry):
        add_chunk(last, c)
        norm_chunk(last, c)

        def dot_body(t, carry):
            at = pl.ds(pl.multiple_of(t * tile, tile), tile)
            out = jnp.dot(r["x"][...], r["w"][last, :, at], preferred_element_type=jnp.float32)
            out = out.astype(jnp.bfloat16).astype(jnp.float32)
            mine = pl.ds(pl.multiple_of(place * cols + t * tile, tile), tile)
            slot = c * part + lax.broadcasted_iota(jnp.int32, (part, tile), 0)
            total = r["stream"][rows_of(c), mine] + out
            total = jnp.where(slot < count, total, 0.0)
            r["mixed"][rows_of(c), at] = total.astype(jnp.bfloat16)
            return carry

        lax.fori_loop(0, tiles, dot_body, 0)
        return carry

    lax.fori_loop(0, chunks, last_body, 0)

    def finish_gather(l, carry):
        for way, hop, sub in all_rings():
            ring_copy(l, way, hop, sub).wait_send()
        for owner, slot, sub in all_mates():
            mate_copy(l, owner, slot, sub).wait_send()
        return carry

    lax.fori_loop(0, layers, finish_gather, 0)

    def finish_layer(l, carry):
        def finish_body(c, carry):
            for hop in range(hops):
                for way in range(2):

                    @pl.when(has_sent(way, hop))
                    def _():
                        pass_on(l, way, hop, c).wait_send()

            return carry

        return lax.fori_loop(0, chunks, finish_body, carry)

    lax.fori_loop(0, layers - 1, finish_layer, 0)


def run_layers(sizes, own, tokens, hot, table, gain, counts):
    n_dp, n = sizes
    layers, rows, cols = own.shape
    tok, width = tokens.shape
    chunks = 4
    part = tok // chunks
    half = n_dp // 4
    dma = pltpu.SemaphoreType.DMA
    names = ["own", "tokens", "hot", "table", "gain", "counts", "mixed"]
    scratch = {
        "w": pltpu.VMEM((layers, n_dp * rows, cols), jnp.bfloat16),
        "stream": pltpu.VMEM((tok, width), jnp.float32),
        "b": pltpu.VMEM((layers - 1, tok, width), jnp.bfloat16),
        "x": pltpu.VMEM((part, width), jnp.bfloat16),
        "own_sem": dma((layers,)),
        "tok_sem": dma((1,)),
        "ring_send": dma((layers, 2, half, 2)),
        "ring_recv": dma((layers, 2, half, 2)),
        "mate_send": dma((layers, 1 + 2 * half, 2)),
        "mate_recv": dma((layers, 1 + 2 * half, 2)),
        "send": dma((layers - 1, 2, n - 1, chunks)),
        "recv": dma((layers - 1, 2, n - 1, chunks)),
    }
    return pl.pallas_call(
        functools.partial(layers_kernel, n_dp, n, chunks, names + list(scratch)),
        out_shape=jax.ShapeDtypeStruct((tok, cols), jnp.bfloat16),
        in_specs=[ANY, ANY, VMEM, VMEM, VMEM, SMEM],
        out_specs=VMEM,
        scratch_shapes=list(scratch.values()),
        compiler_params=pltpu.CompilerParams(
            collective_id=1, has_side_effects=True, vmem_limit_bytes=63 * 2**20
        ),
        name="layers",
    )(own, tokens, hot, table, gain[:, None, :], counts)


def code_table(width):
    quarter = width // 4
    freqs = 1.0 / 10000.0 ** (jnp.arange(quarter, dtype=jnp.float32) / quarter)
    angle = jnp.arange(GRID, dtype=jnp.float32)[:, None] * freqs[None, :]
    exact = jnp.concatenate([jnp.sin(angle), jnp.cos(angle)], axis=1)
    high = lax.reduce_precision(exact, 8, 7)
    middle = lax.reduce_precision(exact - high, 8, 7)
    low = exact - high - middle
    lane = jnp.zeros((GRID, 2 * quarter), jnp.float32)
    rows = jnp.concatenate([high, middle, low, lane], axis=0).astype(jnp.bfloat16)
    empty = jnp.zeros_like(rows)
    return jnp.concatenate(
        [jnp.concatenate([rows, empty], axis=1), jnp.concatenate([empty, rows], axis=1)], axis=0
    )


def one_hot(patch_index):
    lane = lax.broadcasted_iota(jnp.int32, (1, 8 * GRID), 1)
    which = jnp.where(lane < 4 * GRID, patch_index[:, None] // GRID, patch_index[:, None] % GRID)
    return (lane % GRID == which).astype(jnp.bfloat16)


def per_device(
    sizes,
    tokens,
    counts,
    patch_index,
    clip_limit,
    norm_gain,
    params,
    moments,
    seconds,
    gradients,
):
    factor, head = total_over_mesh(sizes, clip_limit, gradients, params, moments, seconds)
    params_new, moments_new, seconds_new, own = adam_all(
        factor, params, moments, seconds, gradients
    )
    table = code_table(tokens.shape[1])
    hot = one_hot(patch_index)
    mixed = run_layers(sizes, own, tokens, hot, table, norm_gain, counts)
    return (params_new, moments_new, seconds_new, mixed)


def solution(mesh):
    sizes = (mesh.shape["dp"], mesh.shape["fsdp"])
    weight = P(None, "dp", "fsdp")
    return jax.shard_map(
        functools.partial(per_device, sizes),
        mesh=mesh,
        in_specs=(P("dp", None), P("dp"), P("dp"), P(), P(), weight, weight, weight, weight),
        out_specs=(weight, weight, weight, P("dp", "fsdp")),
        check_vma=False,
    )
```

time: 346 us -> 309 us (0.89)
  other arithmetic: 52.6 us -> 2.34 us
  Pallas kernels: 261 us -> 301 us
  between operations: 15.9 us -> 2.01 us
  waiting for transfers between devices: 8.56 us -> 0 us
  local copies, waits for them, and re-layouts: 6.94 us -> 3.02 us
    pallas_call x5 -> x3, Pallas kernels: 261 us -> 301 us  [the longest x1 253 us: run_layers(): pl.pallas_call(functools.partial(layers_kernel, n_dp, n, chunks, names +...]
    another operation x1, other arithmetic: 21.4 us -> 0.03 us
    sin x1, other arithmetic: 14.7 us -> 0.25 us  [code_table(): exact = jnp.concatenate([jnp.sin(angle), jnp.cos(angle)], axis=1)]
    all_gather x4 -> x0, waiting for transfers between devices: 8.49 us -> none  [the longest x1 8.43 us: per_device(): weights = lax.all_gather(head, 'dp', axis=0, tiled=True)]
    reduce_sum x1 -> x0, other arithmetic: 6.15 us -> none  [per_device(): squares = total_over_mesh(jnp.sum(gradients * gradients), sizes)]
    convert_element_type x2 -> x1, other arithmetic: 6.2 us -> 0.86 us  [one_hot(): return (lane % GRID == which).astype(jnp.bfloat16)]
    select_n x1 -> x2, other arithmetic: 4.12 us -> 0.01 us  [the longest x1 0.01 us: one_hot(): patch_index[:, None] // GRID]
    convert_element_type x1 -> x0, local copies, waits for them, and re-layouts: 3.84 us -> none  [per_device(): piece = params_new[current + 1].astype(jnp.bfloat16)]
  transfers between devices with their start and end apart: 4 -> 0, of which waited for: 1 -> 0; matrix products, arithmetic and copies ran while one was open for 13% -> 0% of each run, Pallas kernels for 66% -> 0%
where the time goes in v1:
time: 309 us; the launch traced here: 308 us
  Pallas kernels  301 us (97%)
    pallas_call x1, Pallas kernels, run_layers(): pl.pallas_call(functools.partial(layers_kernel, n_dp, n, chunks, names +...  253 us
    pallas_call x1, Pallas kernels, adam_all(): pl.pallas_call(adam_kernel, grid=(layers, rows // part), out_shape=[f32,...  30.3 us
    pallas_call x1, Pallas kernels, total_over_mesh(): pl.pallas_call(functools.partial(total_kernel, sizes, chunks), out_shape=...  17.8 us

profile of v1, /device:TPU:0, one launch (start us, length us, event | category | flops | bytes accessed | tf_op | source)
XLA Modules:
  0.0 308.2 jit_solution(14750789445139798505)
XLA Ops:
  1.3 17.8 %total.1 = (f32[8,128]{1,0:T(8,128)}, bf16[512,1024]{1,0:T(8,128)(2,1)}) custom-call(f32[1]{0:T(128)} %bitcast.1.clip_ref, f32[4,512,1024]{2,1,0:T(8,128)} %g_ref.3, f32[4,512,1024]{2,1,0:T(8,128)} %p_ref.3, f32[4,512,1024]{2,1,0:T(8,128)} %m_ref.3, f32[4,512,1024]{2,1,0:T(8,128)} %s_ref.3), custom_call_target="tpu_custom_call" | custom-call | tf_op jit(solution)/shard_map/total/pallas_call | solution.py:131
  19.0 0.0 copy-start.1
  19.1 0.0 copy-start
  19.1 30.3 %adam.1 = (f32[4,512,1024]{2,1,0:T(8,128)}, f32[4,512,1024]{2,1,0:T(8,128)}, f32[4,512,1024]{2,1,0:T(8,128)}, bf16[4,512,1024]{2,1,0:T(8,128)(2,1)}) custom-call(f32[8,128]{1,0:T(8,128)} %get-tuple-element.9.f_ref, f32[4,512,1024]{2,1,0:T(8,128)} %p_ref.3, f32[4,512,1024]{2,1,0:T(8,128)} %m_ref.3, f32[4,512,1024]{2,1,0:T(8,128)} %s_ref.3, f32[4,512,1024]{2,1,0:T(8,128)} %g_ref.3), custom_call_target="tpu_custom_call" | custom-call | flops 41943040 | bytes 62914560 | tf_op jit(solution)/shard_map/adam/pallas_call | solution.py:170
  49.4 0.0 copy-done.1
  49.4 0.9 fusion.3.refs_2_
  50.3 0.2 fusion.6
  50.6 0.1 pad.7.clone
  50.7 0.1 maximum_maximum_fusion
  50.8 1.1 fusion.2.refs_3_
  51.9 0.0 copy-done
  51.9 0.7 broadcast_in_dim.43.refs_4_
  53.2 252.7 %layers.1 = bf16[512,1024]{1,0:T(8,128)(2,1)} custom-call(bf16[4,512,1024]{2,1,0:T(8,128)(2,1)} %get-tuple-element.13.refs_0_, bf16[512,4096]{1,0:T(8,128)(2,1)} %refs_1_.1, bf16[512,128]{1,0:T(8,128)(2,1)} %fusion.3.refs_2_, bf16[128,4096]{1,0:T(8,128)(2,1)} %fusion.2.refs_3_, f32[4,1,4096]{2,1,0:T(1,128)} %broadcast_in_dim.43.refs_4_, s32[1]{0:T(128)S(6)} %copy.14.refs_5_), custom_call_target="tpu_custom_call" | custom-call | tf_op jit(solution)/shard_map/layers/pallas_call | solution.py:494
  305.9 2.3 copy.16
  (6 shorter events, 0.1 us)
Async XLA Ops:
  19.0 30.3 %copy-start.1 = (s32[512]{0:T(512)S(1)}, s32[512]{0:T(512)}, u32[]{:S(2)}) copy-start(s32[512]{0:T(512)} %param.11) | copy-start | bytes 6148
  19.1 32.8 %copy-start = (f32[4,4096]{1,0:T(4,128)S(1)}, f32[4,4096]{1,0:T(4,128)}, u32[]{:S(2)}) copy-start(f32[4,4096]{1,0:T(4,128)} %param.13) | copy-start | bytes 196612

commit v2 on v1

--- a/solution.py
+++ b/solution.py
@@ -26,8 +26,9 @@
     clipped = gradients * factor
     moments_new = beta_one * moments + (1.0 - beta_one) * clipped
     seconds_new = beta_two * seconds + (1.0 - beta_two) * clipped * clipped
+    spread = seconds_new * (1.0 / (1.0 - beta_two**STEP))
     direction = (moments_new * (1.0 / (1.0 - beta_one**STEP))) / (
-        jnp.sqrt(seconds_new * (1.0 / (1.0 - beta_two**STEP))) + adam_eps
+        spread * lax.rsqrt(spread) + adam_eps
     )
     params_new = params - learning_rate * (direction + weight_decay * params)
     return (params_new, moments_new, seconds_new)
@@ -192,9 +193,18 @@
     ring = n_dp // 2
     half = ring // 2
     hops = n - 1
+    sub = 32
+    split = 2
+    last = layers - 1
     dp, place = lax.axis_index("dp"), lax.axis_index("fsdp")
     chip, core = dp // 2, lax.rem(dp, 2)
     count = r["counts"][0]
+
+    side = place // (n // 2)
+    end = side * (n - 1)
+    middle = n // 2 - 1 + side
+    inner = jnp.logical_and(place > 0, place < n - 1)
+    outer = jnp.logical_not(inner)
 
     def turn(i):
         if ring != 4:
@@ -206,8 +216,8 @@
     def dp_of(position, which):
         return turn(lax.rem(position + 2 * ring, ring)) * 2 + which
 
-    def w_rows(position, which, sub):
-        at = dp_of(position, which) * rows + sub * sub_rows
+    def w_rows(position, sub):
+        at = dp_of(position, core) * rows + sub * sub_rows
         return pl.ds(pl.multiple_of(at, sub_rows), sub_rows)
 
     def rows_of(c):
@@ -215,6 +225,17 @@
 
     def cols_of(owner):
         return pl.ds(pl.multiple_of(owner * cols, cols), cols)
+
+    everything = pl.ds(0, cols)
+    first_cols = cols // 8 * 5
+    by_z = pl.ds(0, first_cols)
+    by_ring = pl.ds(first_cols, cols - first_cols)
+    next_chip = {"dp": dp_of(pos + 1, core)}
+    last_chip = {"dp": dp_of(pos - 1, core)}
+    mate = {"dp": chip * 2 + 1 - core}
+
+    def spare(l):
+        return 0 if l == last else layers + l - split
 
     def take_own(l):
         return pltpu.make_async_copy(
@@ -223,80 +244,159 @@
             r["own_sem"].at[l],
         )
 
-    def ring_copy(l, way, hop, sub):
-        owner = pos - hop if way == 0 else pos + hop
-        at = w_rows(owner, core, sub)
+    def take_near(way):
+        owner = came(way, 0)
+        at = pl.ds(pl.multiple_of(dp_of(owner, core) * rows, rows), rows)
+        return pltpu.make_async_copy(
+            r["from_last" if way == 0 else "from_next"], r["w"].at[0, at], r["near_sem"].at[way]
+        )
+
+    def send_rows(to, source, target, owner, sub, which, send, recv):
+        at = w_rows(owner, sub)
         return pltpu.make_async_remote_copy(
-            src_ref=r["w"].at[l, at],
-            dst_ref=r["w"].at[l, at],
-            send_sem=r["ring_send"].at[l, way, hop, sub],
-            recv_sem=r["ring_recv"].at[l, way, hop, sub],
-            device_id={"dp": dp_of(pos + 1 if way == 0 else pos - 1, core)},
+            src_ref=r["w"].at[source, at, which],
+            dst_ref=r["w"].at[target, at, which],
+            send_sem=send,
+            recv_sem=recv,
+            device_id=to,
             device_id_type=MESH,
         )
 
-    def mate_copy(l, owner, slot, sub):
-        at = w_rows(owner, core, sub)
-        return pltpu.make_async_remote_copy(
-            src_ref=r["w"].at[l, at],
-            dst_ref=r["w"].at[l, at],
-            send_sem=r["mate_send"].at[l, slot, sub],
-            recv_sem=r["mate_recv"].at[l, slot, sub],
-            device_id={"dp": chip * 2 + 1 - core},
-            device_id_type=MESH,
-        )
-
     def came(way, hop):
         return pos - 1 - hop if way == 0 else pos + 1 + hop
 
-    def all_mates():
-        out = [(pos, 0, 0), (pos, 0, 1)]
-        for hop in range(half):
-            for way in range(2):
-                for sub in range(2):
-                    if hop < half - 1 or sub == way:
-                        out.append((came(way, hop), 1 + 2 * hop + way, sub))
-        return out
-
-    def all_rings():
-        out = []
-        for hop in range(half):
-            for way in range(2):
-                for sub in range(2):
-                    if hop < half - 1 or sub == way:
-                        out.append((way, hop, sub))
-        return out
-
     ring_order = ((0, 0), (1, 1), (0, 1), (1, 0))
 
-    def gather_start(l):
-        take_own(l).wait()
-        for way, sub in ring_order:
-            if half > 1 or sub == way:
-                ring_copy(l, way, 0, sub).start()
-        for sub in range(2):
-            mate_copy(l, pos, 0, sub).start()
-
-    def gather_mid(l):
-        for hop in range(half - 1):
-            for way, sub in ring_order:
-                ring_copy(l, way, hop, sub).wait_recv()
-                if hop + 1 < half - 1 or sub == way:
-                    ring_copy(l, way, hop + 1, sub).start()
-                mate_copy(l, came(way, hop), 1 + 2 * hop + way, sub).start()
-
-    def gather_end(l):
-        hop = half - 1
-        for way in range(2):
-            ring_copy(l, way, hop, way).wait_recv()
-            mate_copy(l, came(way, hop), 1 + 2 * hop + way, way).start()
-        for owner, slot, sub in all_mates():
-            mate_copy(l, owner, slot, sub).wait_recv()
+    def arrivals(hop):
+        return [(way, sub) for way, sub in ring_order if hop < half - 1 or sub == way]
+
+    class Gather:
+        def __init__(self, slot, index, which):
+            self.slot, self.index, self.which = slot, index, which
+
+        def ring(self, way, hop, sub):
+            at = (self.index, way, hop, sub)
+            return send_rows(
+                next_chip if way == 0 else last_chip,
+                self.slot,
+                self.slot,
+                pos - hop if way == 0 else pos + hop,
+                sub,
+                self.which,
+                r["ring_send"].at[at],
+                r["ring_recv"].at[at],
+            )
+
+        def mate(self, owner, slot, sub):
+            at = (self.index, slot, sub)
+            return send_rows(
+                mate,
+                self.slot,
+                self.slot,
+                owner,
+                sub,
+                self.which,
+                r["mate_send"].at[at],
+                r["mate_recv"].at[at],
+            )
+
+        def blocks(self):
+            out = [(pos, 0, 0), (pos, 0, 1)]
+            for hop in range(half):
+                out += [(came(way, hop), 1 + 2 * hop + way, sub) for way, sub in arrivals(hop)]
+            return out
+
+        def start_ring(self):
+            for way, sub in arrivals(0):
+                self.ring(way, 0, sub).start()
+
+        def start(self):
+            self.start_ring()
+            for sub in range(2):
+                self.mate(pos, 0, sub).start()
+
+        def step(self, hop, relay, arrived=None):
+            for way, sub in arrivals(hop):
+                if arrived is None:
+                    self.ring(way, hop, sub).wait_recv()
+                elif sub == way:
+                    arrived(way)
+                if hop + 1 < half and (way, sub) in arrivals(hop + 1):
+                    self.ring(way, hop + 1, sub).start()
+                if relay is not None:
+                    relay(came(way, hop), 1 + 2 * hop + way, sub).start()
+
+        def mid(self, relay=None):
+            for hop in range(half - 1):
+                self.step(hop, relay or self.mate)
+
+        def finish(self, relay=None):
+            self.step(half - 1, relay or self.mate)
+
+        def wait_mates(self):
+            for owner, slot, sub in self.blocks():
+                self.mate(owner, slot, sub).wait_recv()
+
+        def end(self):
+            self.finish()
+            self.wait_mates()
+
+        def sent_ring(self, first=0):
+            for hop in range(first, half):
+                for way, sub in arrivals(hop):
+                    self.ring(way, hop, sub).wait_send()
+
+        def sent_mates(self):
+            for owner, slot, sub in self.blocks():
+                self.mate(owner, slot, sub).wait_send()
+
+    class Across(Gather):
+        def __init__(self, l):
+            self.l, self.to = l, {"fsdp": middle}
+            self.a = Gather(spare(l), layers + l - split, by_z)
+            self.b = Gather(spare(l), layers + l - split, by_ring)
+            self.out = Gather(l, layers + l - split, by_ring)
+
+        def sems(self, slot, sub):
+            at = (self.l - split, slot, sub)
+            return r["across_send"].at[at], r["across_recv"].at[at]
+
+        def first(self, sub):
+            pair = self.sems(ring + 1, sub)
+            return send_rows(self.to, self.l, spare(self.l), pos, sub, by_z, *pair)
+
+        def open_first(self):
+            for sub in range(2):
+                self.first(sub).start()
+
+        def relay_own(self):
+            for sub in range(2):
+                self.relay(pos, 0, sub).start()
+
+        def relay(self, owner, slot, sub):
+            pair = self.sems(slot, sub)
+            return send_rows(self.to, self.l, spare(self.l), owner, sub, by_ring, *pair)
+
+        def mate_b(self, owner, slot, sub):
+            at = (self.l - split, slot, sub)
+            return send_rows(
+                mate,
+                spare(self.l),
+                spare(self.l),
+                owner,
+                sub,
+                by_ring,
+                r["again_send"].at[at],
+                r["again_recv"].at[at],
+            )
+
+    gathers = [Gather(l, l, everything) for l in range(layers)]
+    across = {l: Across(l) for l in range(split, layers)}
 
     def pass_on(l, way, hop, c):
         owner = place - hop if way == 0 else place + hop
         peer = lax.rem(place + 1, n) if way == 0 else lax.rem(place + n - 1, n)
-        target = r["b"].at[l, rows_of(c), cols_of(owner)]
+        target = r["b"].at[l % 2, rows_of(c), cols_of(owner)]
         return pltpu.make_async_remote_copy(
             src_ref=target,
             dst_ref=target,
@@ -306,43 +406,81 @@
             device_id_type=MESH,
         )
 
-    def has_sent(way, hop):
+    def has_sent(l, way, hop):
         if way == 0:
-            return jnp.logical_and(place < n - 1, place >= hop)
-        return jnp.logical_and(place > 0, place + hop < n)
-
-    def has_got(way, hop):
-        return place >= hop + 1 if way == 0 else place + hop + 1 < n
-
-    take_tokens = pltpu.make_async_copy(r["tokens"], r["b"].at[layers - 2], r["tok_sem"].at[0])
-    take_tokens.start()
+            near = place < (n - 1 if l + 1 < split else n - 2)
+            far = place >= hop
+        else:
+            near = place > (0 if l + 1 < split else 1)
+            far = place + hop < n
+        both = jnp.logical_and(near, far)
+        return jnp.logical_and(both, inner) if l >= split else both
+
+    def has_got(l, way, hop):
+        if way == 0:
+            near = place <= (n - 1 if l + 1 < split else n - 2)
+            far = place >= hop + 1
+        else:
+            near = place >= (0 if l + 1 < split else 1)
+            far = place + hop + 1 < n
+        both = jnp.logical_and(near, far)
+        if l >= split:
+            both = jnp.logical_and(both, place >= n // 2 if way == 0 else place < n // 2)
+            both = jnp.logical_and(both, inner)
+        return both
+
+    def give_mixed(c):
+        return pltpu.make_async_remote_copy(
+            src_ref=r["b"].at[1, rows_of(c), cols_of(end)],
+            dst_ref=r["mixed"].at[rows_of(c)],
+            send_sem=r["mixed_send"].at[c],
+            recv_sem=r["mixed_recv"].at[c],
+            device_id={"fsdp": jnp.where(inner, end, middle)},
+            device_id_type=MESH,
+        )
+
+    take_tokens = pltpu.make_async_copy(r["tokens"], r["b"].at[1], r["tok_sem"].at[0])
     for l in range(layers):
         take_own(l).start()
+    for way in range(2):
+        take_near(way).start()
+    take_tokens.start()
 
     barrier = pltpu.get_barrier_semaphore()
     peers = [{"fsdp": lax.rem(place + 1, n)}, {"fsdp": lax.rem(place + n - 1, n)}]
-    peers += [{"dp": dp_of(pos + 1, core)}, {"dp": dp_of(pos - 1, core)}]
-    peers += [{"dp": chip * 2 + 1 - core}]
+    peers += [next_chip, last_chip, mate]
     for peer in peers:
         pl.semaphore_signal(barrier, inc=1, device_id=peer, device_id_type=MESH)
     pl.semaphore_wait(barrier, len(peers))
 
-    gather_start(0)
+    for l in range(layers):
+        take_own(l).wait()
+    opening = gathers[0]
+    opening.step(0, opening.mate, lambda way: take_near(way).wait())
+    for half_block in range(2):
+        opening.mate(pos, 0, half_block).start()
+    gathers[1].start()
+
+    @pl.when(outer)
+    def _():
+        across[split].open_first()
+
     take_tokens.wait()
 
     def init_body(t, carry):
         at = pl.ds(pl.multiple_of(t * tile, tile), tile)
         code = jnp.dot(r["hot"][...], r["table"][:, at], preferred_element_type=jnp.float32)
         slot = lax.broadcasted_iota(jnp.int32, code.shape, 0)
-        value = r["b"][layers - 2, :, at].astype(jnp.float32) + code
+        value = r["b"][1, :, at].astype(jnp.float32) + code
         r["stream"][:, at] = jnp.where(slot < count, value, 0.0)
         return carry
 
-    lax.fori_loop(0, width // tile, init_body, 0)
-    gather_mid(0)
-    gather_end(0)
-
-    sub = 32
+    with jax.named_scope("init"):
+        lax.fori_loop(0, width // tile, init_body, 0)
+    with jax.named_scope("opening"):
+        for hop in range(1, half - 1):
+            opening.step(hop, opening.mate)
+        opening.end()
 
     def norm_chunk(l, c):
         def norm_body(k, carry):
@@ -352,123 +490,264 @@
             shifted = x - centre
             spread = jnp.sum(shifted * shifted, axis=1, keepdims=True) * (1.0 / width)
             normed = shifted * lax.rsqrt(spread + norm_eps) * r["gain"][l]
-            r["x"][pl.ds(pl.multiple_of(k * sub, sub), sub)] = normed.astype(jnp.bfloat16)
+            r["x"][at] = normed.astype(jnp.bfloat16)
             return carry
 
         lax.fori_loop(0, part // sub, norm_body, 0)
 
     def add_chunk(l, c):
-        for way in range(2):
-
-            @pl.when(has_got(way, hops - 1))
-            def _():
-                pass_on(l - 1, way, hops - 1, c).wait_recv()
-
         def add_body(k, carry):
             at = pl.ds(pl.multiple_of(c * part + k * sub, sub), sub)
-            r["stream"][at] = r["stream"][at] + r["b"][l - 1, at].astype(jnp.float32)
+            r["stream"][at] = r["stream"][at] + r["b"][(l - 1) % 2, at].astype(jnp.float32)
             return carry
 
         lax.fori_loop(0, part // sub, add_body, 0)
 
-    def layer_body(l, carry):
-        gather_start(l + 1)
-
-        def chunk_body(c, carry):
-            @pl.when(l > 0)
+    def wait_pieces(l, hop, c):
+        for way in range(2):
+
+            @pl.when(has_got(l, way, hop))
             def _():
-                add_chunk(l, c)
-
-            norm_chunk(l, c)
-
-            def dot_body(t, carry):
-                at = pl.ds(pl.multiple_of(t * tile, tile), tile)
-                out = jnp.dot(r["x"][...], r["w"][l, :, at], preferred_element_type=jnp.float32)
-                mine = pl.ds(pl.multiple_of(place * cols + t * tile, tile), tile)
-                r["b"][l, rows_of(c), mine] = out.astype(jnp.bfloat16)
-                return carry
-
-            lax.fori_loop(0, tiles, dot_body, 0)
-            for way in range(2):
-
-                @pl.when(has_sent(way, 0))
-                def _():
-                    pass_on(l, way, 0, c).start()
-
-            return carry
-
-        lax.fori_loop(0, chunks, chunk_body, 0)
-        for hop in range(hops - 1):
-
-            def forward_body(c, carry):
-                for way in range(2):
-
-                    @pl.when(has_got(way, hop))
-                    def _():
-                        pass_on(l, way, hop, c).wait_recv()
-
-                    @pl.when(has_sent(way, hop + 1))
-                    def _():
-                        pass_on(l, way, hop + 1, c).start()
-
-                return carry
-
-            lax.fori_loop(0, chunks, forward_body, 0)
-            if hop == 0:
-                gather_mid(l + 1)
-        gather_end(l + 1)
-        return carry
-
-    lax.fori_loop(0, layers - 1, layer_body, 0)
-
-    last = layers - 1
-
-    def last_body(c, carry):
-        add_chunk(last, c)
-        norm_chunk(last, c)
-
+                pass_on(l, way, hop, c).wait_recv()
+
+    def send_piece(l, hop, c):
+        for way in range(2):
+
+            @pl.when(has_sent(l, way, hop))
+            def _():
+                pass_on(l, way, hop, c).start()
+
+    def multiply(slot, at_rows, take):
         def dot_body(t, carry):
             at = pl.ds(pl.multiple_of(t * tile, tile), tile)
-            out = jnp.dot(r["x"][...], r["w"][last, :, at], preferred_element_type=jnp.float32)
-            out = out.astype(jnp.bfloat16).astype(jnp.float32)
-            mine = pl.ds(pl.multiple_of(place * cols + t * tile, tile), tile)
-            slot = c * part + lax.broadcasted_iota(jnp.int32, (part, tile), 0)
-            total = r["stream"][rows_of(c), mine] + out
-            total = jnp.where(slot < count, total, 0.0)
-            r["mixed"][rows_of(c), at] = total.astype(jnp.bfloat16)
+            out = jnp.dot(
+                r["x"][at_rows], r["w"][slot, :, at], preferred_element_type=jnp.float32
+            )
+            take(t, at, out.astype(jnp.bfloat16))
             return carry
 
         lax.fori_loop(0, tiles, dot_body, 0)
-        return carry
-
-    lax.fori_loop(0, chunks, last_body, 0)
-
-    def finish_gather(l, carry):
-        for way, hop, sub in all_rings():
-            ring_copy(l, way, hop, sub).wait_send()
-        for owner, slot, sub in all_mates():
-            mate_copy(l, owner, slot, sub).wait_send()
-        return carry
-
-    lax.fori_loop(0, layers, finish_gather, 0)
-
-    def finish_layer(l, carry):
-        def finish_body(c, carry):
+
+    def branch_into(l, c, owner):
+        def take(t, at, out):
+            mine = pl.ds(pl.multiple_of(owner * cols + t * tile, tile), tile)
+            r["b"][l % 2, rows_of(c), mine] = out
+
+        return take
+
+    def branch(l, slot, c, owner):
+        multiply(slot, rows_of(c), branch_into(l, c, owner))
+
+    def result(slot, at_rows, start, owner, put):
+        def take(t, at, out):
+            mine = pl.ds(pl.multiple_of(owner * cols + t * tile, tile), tile)
+            place_of = start + lax.broadcasted_iota(jnp.int32, out.shape, 0)
+            total = r["stream"][at_rows, mine] + out.astype(jnp.float32)
+            put(mine, at, jnp.where(place_of < count, total, 0.0).astype(jnp.bfloat16))
+
+        multiply(slot, at_rows, take)
+
+    def over_chunks(body, low=0, high=chunks):
+        lax.fori_loop(low, high, lambda c, carry: (body(c), carry)[1], 0)
+
+    def sent_chunk(l, c):
+        for hop in range(hops):
+            for way in range(2):
+
+                @pl.when(has_sent(l, way, hop))
+                def _():
+                    pass_on(l, way, hop, c).wait_send()
+
+    def sent_pieces(l):
+        over_chunks(lambda c: sent_chunk(l, c))
+
+    @pl.when(outer)
+    def _():
+        across[split].out.start_ring()
+
+    def body(c):
+        norm_chunk(0, c)
+        branch(0, 0, c, place)
+        send_piece(0, 0, c)
+
+    with jax.named_scope("layer_0"):
+        over_chunks(body)
+    opening.sent_ring(1)
+    opening.sent_mates()
+
+    @pl.when(inner)
+    def _():
+        for peer in (next_chip, last_chip, mate, {"fsdp": end}):
+            pl.semaphore_signal(r["free"], inc=1, device_id=peer, device_id_type=MESH)
+
+    def forward(l, hop, low=0, high=chunks):
+        def body(c):
+            if l + 1 == split:
+                sent_chunk(l - 1, c)
+            wait_pieces(l, hop, c)
+            send_piece(l, hop + 1, c)
+
+        over_chunks(body, low, high)
+
+    def layer_one(c):
+        add_chunk(1, c)
+        norm_chunk(1, c)
+        branch(1, 1, c, place)
+        send_piece(1, 0, c)
+
+    both_halves = range(2)
+
+    @pl.when(outer)
+    def _():
+        with jax.named_scope("outer_gather"):
+            gathers[1].mid()
+        with jax.named_scope("outer_feed"):
+            across[split].relay_own()
+            across[split].out.mid(across[split].relay)
+            gathers[1].finish()
+            across[split].out.finish(across[split].relay)
+            across[last].out.start_ring()
+            pl.semaphore_wait(r["free"], 1)
+            gathers[1].wait_mates()
+
+        def body(c):
             for hop in range(hops):
-                for way in range(2):
-
-                    @pl.when(has_sent(way, hop))
-                    def _():
-                        pass_on(l, way, hop, c).wait_send()
-
-            return carry
-
-        return lax.fori_loop(0, chunks, finish_body, carry)
-
-    lax.fori_loop(0, layers - 1, finish_layer, 0)
-
-
-def run_layers(sizes, own, tokens, hot, table, gain, counts):
+                wait_pieces(0, hop, c)
+            layer_one(c)
+
+        with jax.named_scope("outer_layer_1"):
+            over_chunks(body)
+        with jax.named_scope("outer_sent"):
+            sent_pieces(1)
+        with jax.named_scope("outer_feeds"):
+            across[last].open_first()
+            across[last].relay_own()
+            across[last].out.mid(across[last].relay)
+            across[last].out.finish(across[last].relay)
+        with jax.named_scope("outer_mixed"):
+            over_chunks(lambda c: give_mixed(c).wait_recv())
+        for l in range(split, layers):
+            for half_block in both_halves:
+                across[l].first(half_block).wait_send()
+            across[l].out.sent_ring()
+            for owner, slot, half_block in across[l].out.blocks():
+                across[l].relay(owner, slot, half_block).wait_send()
+        sent_pieces(0)
+
+    def open_spare(l):
+        if l == last:
+            pl.semaphore_wait(r["free"], 3)
+        for half_block in both_halves:
+            across[l].first(half_block).wait_recv()
+        across[l].a.start()
+
+    def relay_spare(l):
+        blocks = across[l].b.blocks()
+        for owner, slot, half_block in blocks:
+            across[l].relay(owner, slot, half_block).wait_recv()
+            across[l].mate_b(owner, slot, half_block).start()
+
+    def wait_spare(l):
+        across[l].a.wait_mates()
+        for owner, slot, half_block in across[l].b.blocks():
+            across[l].mate_b(owner, slot, half_block).wait_recv()
+
+    @pl.when(inner)
+    def _():
+        with jax.named_scope("forward_0"):
+            forward(0, 0, 0, chunks - 1)
+        with jax.named_scope("gather_1_mid"):
+            gathers[1].mid()
+        with jax.named_scope("forward_0b"):
+            forward(0, 0, chunks - 1, chunks)
+        with jax.named_scope("forward_1"):
+            forward(0, 1, 0, chunks // 2)
+        gathers[split].start()
+        open_spare(split)
+        with jax.named_scope("forward_1b"):
+            forward(0, 1, chunks // 2, chunks)
+        with jax.named_scope("gather_1_end"):
+            gathers[1].end()
+        with jax.named_scope("layer_1"):
+            over_chunks(layer_one)
+        with jax.named_scope("gather_2_mid"):
+            gathers[split].mid()
+            across[split].a.mid()
+        with jax.named_scope("forward_2"):
+            forward(1, 0, 0, chunks // 2)
+        with jax.named_scope("spare_relay"):
+            relay_spare(split)
+        with jax.named_scope("forward_2b"):
+            forward(1, 0, chunks // 2, chunks)
+        gathers[last].start()
+        with jax.named_scope("gather_2_end"):
+            gathers[split].finish()
+            across[split].a.finish()
+        with jax.named_scope("spare_open"):
+            open_spare(last)
+        with jax.named_scope("wait_mates"):
+            gathers[split].wait_mates()
+            wait_spare(split)
+
+        def body(c):
+            wait_pieces(1, 1, c)
+            add_chunk(split, c)
+            norm_chunk(split, c)
+            branch(split, split, c, place)
+            send_piece(split, 0, c)
+            branch(split, spare(split), c, end)
+            send_piece(split, 1, c)
+
+        with jax.named_scope("layer_2"):
+            over_chunks(body)
+        with jax.named_scope("last_mid"):
+            across[last].a.mid()
+            gathers[last].mid()
+        with jax.named_scope("last_relay"):
+            relay_spare(last)
+        with jax.named_scope("last_spare"):
+            across[last].a.finish()
+            wait_spare(last)
+            sent_pieces(1)
+
+        def put_away(c):
+            def put(mine, at, value):
+                r["b"][1, rows_of(c), mine] = value
+
+            return put
+
+        def put_here(mine, at, value):
+            r["mixed"][:, at] = value
+
+        def body(c):
+            wait_pieces(last - 1, 0, c)
+            wait_pieces(last - 1, 1, c)
+            add_chunk(last, c)
+            norm_chunk(last, c)
+            result(spare(last), rows_of(c), c * part, end, put_away(c))
+            give_mixed(c).start()
+
+        with jax.named_scope("layer_3"):
+            over_chunks(body)
+        with jax.named_scope("last_gather_end"):
+            gathers[last].end()
+        with jax.named_scope("layer_3_own"):
+            result(last, pl.ds(0, tok), 0, place, put_here)
+        sent_pieces(last - 1)
+        for l in range(split, layers):
+            gathers[l].sent_ring()
+            gathers[l].sent_mates()
+            across[l].a.sent_ring()
+            across[l].a.sent_mates()
+            for owner, slot, half_block in across[l].b.blocks():
+                across[l].mate_b(owner, slot, half_block).wait_send()
+        over_chunks(lambda c: give_mixed(c).wait_send())
+
+    gathers[1].sent_ring()
+    gathers[1].sent_mates()
+
+
+def run_layers(sizes, own, from_last, from_next, tokens, hot, table, gain, counts):
     n_dp, n = sizes
     layers, rows, cols = own.shape
     tok, width = tokens.shape
@@ -476,32 +755,50 @@
     part = tok // chunks
     half = n_dp // 4
     dma = pltpu.SemaphoreType.DMA
-    names = ["own", "tokens", "hot", "table", "gain", "counts", "mixed"]
+    names = ["own", "from_last", "from_next", "tokens", "hot", "table", "gain", "counts", "mixed"]
     scratch = {
-        "w": pltpu.VMEM((layers, n_dp * rows, cols), jnp.bfloat16),
+        "w": pltpu.VMEM((layers + 1, n_dp * rows, cols), jnp.bfloat16),
         "stream": pltpu.VMEM((tok, width), jnp.float32),
-        "b": pltpu.VMEM((layers - 1, tok, width), jnp.bfloat16),
-        "x": pltpu.VMEM((part, width), jnp.bfloat16),
+        "b": pltpu.VMEM((2, tok, width), jnp.bfloat16),
+        "x": pltpu.VMEM((tok, width), jnp.bfloat16),
         "own_sem": dma((layers,)),
+        "near_sem": dma((2,)),
         "tok_sem": dma((1,)),
-        "ring_send": dma((layers, 2, half, 2)),
-        "ring_recv": dma((layers, 2, half, 2)),
-        "mate_send": dma((layers, 1 + 2 * half, 2)),
-        "mate_recv": dma((layers, 1 + 2 * half, 2)),
+        "ring_send": dma((layers + 2, 2, half, 2)),
+        "ring_recv": dma((layers + 2, 2, half, 2)),
+        "mate_send": dma((layers + 2, 1 + 2 * half, 2)),
+        "mate_recv": dma((layers + 2, 1 + 2 * half, 2)),
+        "across_send": dma((2, 2 + 2 * half, 2)),
+        "across_recv": dma((2, 2 + 2 * half, 2)),
+        "again_send": dma((2, 1 + 2 * half, 2)),
+        "again_recv": dma((2, 1 + 2 * half, 2)),
         "send": dma((layers - 1, 2, n - 1, chunks)),
         "recv": dma((layers - 1, 2, n - 1, chunks)),
+        "mixed_send": dma((chunks,)),
+        "mixed_recv": dma((chunks,)),
+        "free": pltpu.SemaphoreType.REGULAR,
     }
     return pl.pallas_call(
         functools.partial(layers_kernel, n_dp, n, chunks, names + list(scratch)),
         out_shape=jax.ShapeDtypeStruct((tok, cols), jnp.bfloat16),
-        in_specs=[ANY, ANY, VMEM, VMEM, VMEM, SMEM],
+        in_specs=[ANY, ANY, ANY, ANY, VMEM, VMEM, VMEM, SMEM],
         out_specs=VMEM,
         scratch_shapes=list(scratch.values()),
         compiler_params=pltpu.CompilerParams(
-            collective_id=1, has_side_effects=True, vmem_limit_bytes=63 * 2**20
+            collective_id=1, has_side_effects=True, vmem_limit_bytes=67043328
         ),
         name="layers",
-    )(own, tokens, hot, table, gain[:, None, :], counts)
+    )(own, from_last, from_next, tokens, hot, table, gain[:, None, :], counts)
+
+
+def ring_pairs(n_dp):
+    ring = n_dp // 2
+    order = [0, 1, 3, 2] if ring == 4 else list(range(ring))
+    return [
+        (2 * order[i] + core, 2 * order[(i + 1) % ring] + core)
+        for i in range(ring)
+        for core in range(2)
+    ]
 
 
 def code_table(width):
@@ -539,12 +836,17 @@
     gradients,
 ):
     factor, head = total_over_mesh(sizes, clip_limit, gradients, params, moments, seconds)
+    pairs = ring_pairs(sizes[0])
+    from_last = lax.ppermute(head, "dp", pairs)
+    from_next = lax.ppermute(head, "dp", [(target, source) for source, target in pairs])
     params_new, moments_new, seconds_new, own = adam_all(
         factor, params, moments, seconds, gradients
     )
     table = code_table(tokens.shape[1])
     hot = one_hot(patch_index)
-    mixed = run_layers(sizes, own, tokens, hot, table, norm_gain, counts)
+    mixed = run_layers(
+        sizes, own, from_last, from_next, tokens, hot, table, norm_gain, counts
+    )
     return (params_new, moments_new, seconds_new, mixed)
 
 

time: 309 us -> 249 us (0.81)
  Pallas kernels: 301 us -> 240 us
    pallas_call x1, Pallas kernels: 253 us -> 193 us  [run_layers(): pl.pallas_call(functools.partial(layers_kernel, n_dp, n, chunks, names +...]
  transfers between devices with their start and end apart: 0 -> 2, of which waited for: 0 -> 0; matrix products, arithmetic and copies ran while one was open for 0% -> 1% of each run, Pallas kernels for 0% -> 12%
where the time goes in v2:
time: 249 us
  Pallas kernels  240 us (96%)
  local copies, waits for them, and re-layouts  3.02 us (1%)
    pallas_call x1, Pallas kernels, run_layers(): pl.pallas_call(functools.partial(layers_kernel, n_dp, n, chunks, names +...  193 us
    pallas_call x1, Pallas kernels, adam_all(): pl.pallas_call(adam_kernel, grid=(layers, rows // part), out_shape=[f32,...  29.1 us
    pallas_call x1, Pallas kernels, total_over_mesh(): pl.pallas_call(functools.partial(total_kernel, sizes, chunks), out_shape=...  17.5 us
  transfers between devices with their start and end apart: 2, of which 0 were waited for; matrix products, arithmetic and copies ran while one was open for 1% of the time, Pallas kernels for 12%

profile of v2, /device:TPU:0, one launch (start us, length us, event | category | flops | bytes accessed | tf_op | source)
XLA Modules:
  0.0 249.0 jit_solution(14716813827567058829)
XLA Ops:
  1.3 17.5 %total.1 = (f32[8,128]{1,0:T(8,128)}, bf16[512,1024]{1,0:T(8,128)(2,1)}) custom-call(f32[1]{0:T(128)} %bitcast.1.clip_ref, f32[4,512,1024]{2,1,0:T(8,128)} %g_ref.3, f32[4,512,1024]{2,1,0:T(8,128)} %p_ref.3, f32[4,512,1024]{2,1,0:T(8,128)} %m_ref.3, f32[4,512,1024]{2,1,0:T(8,128)} %s_ref.3), custom_call_target="tpu_custom_call" | custom-call | tf_op jit(solution)/shard_map/total/pallas_call | solution.py:132
  18.8 0.7 collective-permute-start
  19.5 1.4 collective-permute-start.1
  20.9 0.0 copy-start.1
  20.9 0.0 copy-start
  20.9 29.1 %adam.1 = (f32[4,512,1024]{2,1,0:T(8,128)}, f32[4,512,1024]{2,1,0:T(8,128)}, f32[4,512,1024]{2,1,0:T(8,128)}, bf16[4,512,1024]{2,1,0:T(8,128)(2,1)}) custom-call(f32[8,128]{1,0:T(8,128)} %get-tuple-element.10.f_ref, f32[4,512,1024]{2,1,0:T(8,128)} %p_ref.3, f32[4,512,1024]{2,1,0:T(8,128)} %m_ref.3, f32[4,512,1024]{2,1,0:T(8,128)} %s_ref.3, f32[4,512,1024]{2,1,0:T(8,128)} %g_ref.3), custom_call_target="tpu_custom_call" | custom-call | flops 41943040 | bytes 62914560 | tf_op jit(solution)/shard_map/adam/pallas_call | solution.py:171
  50.0 0.0 copy-done.1
  50.0 0.2 fusion.6
  50.3 0.0 copy-done
  50.3 0.7 broadcast_in_dim.43.refs_6_
  51.7 0.1 pad.7.clone
  51.7 0.9 fusion.3.refs_4_
  52.6 0.1 maximum_maximum_fusion
  52.7 1.1 fusion.2.refs_5_
  53.8 0.0 collective-permute-done.refs_1_
  53.8 0.0 collective-permute-done.1.refs_2_
  53.8 192.9 %layers.1 = bf16[512,1024]{1,0:T(8,128)(2,1)} custom-call(bf16[4,512,1024]{2,1,0:T(8,128)(2,1)} %get-tuple-element.14.refs_0_, bf16[512,1024]{1,0:T(8,128)(2,1)} %collective-permute-done.refs_1_, bf16[512,1024]{1,0:T(8,128)(2,1)} %collective-permute-done.1.refs_2_, bf16[512,4096]{1,0:T(8,128)(2,1)} %refs_3_.1, bf16[512,128]{1,0:T(8,128)(2,1)} %fusion.3.refs_4_, ...), custom_call_target="tpu_custom_call" | custom-call | tf_op jit(solution)/shard_map/layers/pallas_call | solution.py:781
  246.7 2.3 copy.16
  (6 shorter events, 0.1 us)
Async XLA Ops:
  18.8 34.9 %collective-permute-start = (bf16[512,1024]{1,0:T(8,128)(2,1)}, bf16[512,1024]{1,0:T(8,128)(2,1)}, u32[]{:S(2)}, u32[]{:S(2)}) collective-permute-start(bf16[512,1024]{1,0:T(8,128)(2,1)} %get-tuple-element.15), channel_id=1, source_target_pairs={{0,8},{4,12},{8,24},{12,28},{24,16},{28,20},{16,0},{20,4},{1,9},{5... | collective-permute-start | bytes 3145736 | tf_op jit(solution)/shard_map/ppermute | solution.py:840
  19.5 34.2 %collective-permute-start.1 = (bf16[512,1024]{1,0:T(8,128)(2,1)}, bf16[512,1024]{1,0:T(8,128)(2,1)}, u32[]{:S(2)}, u32[]{:S(2)}) collective-permute-start(bf16[512,1024]{1,0:T(8,128)(2,1)} %get-tuple-element.15), channel_id=1, source_target_pairs={{8,0},{12,4},{24,8},{28,12},{16,24},{20,28},{0,16},{4,20},{9,1},{1... | collective-permute-start | bytes 3145736 | tf_op jit(solution)/shard_map/ppermute | solution.py:841
  20.9 29.1 %copy-start.1 = (s32[512]{0:T(512)S(1)}, s32[512]{0:T(512)}, u32[]{:S(2)}) copy-start(s32[512]{0:T(512)} %param.11) | copy-start | bytes 6148
  20.9 29.3 %copy-start = (f32[4,4096]{1,0:T(4,128)S(1)}, f32[4,4096]{1,0:T(4,128)}, u32[]{:S(2)}) copy-start(f32[4,4096]{1,0:T(4,128)} %param.13) | copy-start | bytes 196612

commit v3 on v2

--- a/solution.py
+++ b/solution.py
@@ -82,13 +82,15 @@
 
         return lax.fori_loop(0, chunks, add_chunk, total)
 
-    wide = lax.fori_loop(0, layers, add_layer, jnp.zeros((8, cols), jnp.float32))
+    with jax.named_scope("add_up"):
+        wide = lax.fori_loop(0, layers, add_layer, jnp.zeros((8, cols), jnp.float32))
     total = wide[:, 0:128]
     for k in range(1, cols // 128):
         total = total + wide[:, 128 * k : 128 * k + 128]
     mine[...] = total
 
-    pl.semaphore_wait(barrier, sizes[0] + sizes[1] - 2)
+    with jax.named_scope("total_barrier"):
+        pl.semaphore_wait(barrier, sizes[0] + sizes[1] - 2)
     for axis in range(2):
         source = mine if axis == 0 else mid
         copies = []
@@ -122,7 +124,8 @@
         head_ref[at] = adam_update(p[at], m[at], s[at], g[0, at], factor)[0].astype(jnp.bfloat16)
         return carry
 
-    lax.fori_loop(0, rows // 16, update, 0)
+    with jax.named_scope("head_update"):
+        lax.fori_loop(0, rows // 16, update, 0)
 
 
 def total_over_mesh(sizes, clip_limit, gradients, params, moments, seconds):
@@ -165,7 +168,7 @@
 
 def adam_all(factor, params, moments, seconds, gradients):
     layers, rows, cols = params.shape
-    part = 128
+    part = min(512, rows)
     block = pl.BlockSpec((1, part, cols), lambda l, c: (l, c, 0))
     f32 = jax.ShapeDtypeStruct(params.shape, jnp.float32)
     return pl.pallas_call(
@@ -227,9 +230,16 @@
         return pl.ds(pl.multiple_of(owner * cols, cols), cols)
 
     everything = pl.ds(0, cols)
-    first_cols = cols // 8 * 5
-    by_z = pl.ds(0, first_cols)
-    by_ring = pl.ds(first_cols, cols - first_cols)
+
+    def first_cols(l):
+        return cols // 8 * (4 if l == last else 5)
+
+    def by_z(l):
+        return pl.ds(0, first_cols(l))
+
+    def by_ring(l):
+        return pl.ds(first_cols(l), cols - first_cols(l))
+
     next_chip = {"dp": dp_of(pos + 1, core)}
     last_chip = {"dp": dp_of(pos - 1, core)}
     mate = {"dp": chip * 2 + 1 - core}
@@ -306,12 +316,12 @@
                 out += [(came(way, hop), 1 + 2 * hop + way, sub) for way, sub in arrivals(hop)]
             return out
 
-        def start_ring(self):
-            for way, sub in arrivals(0):
+        def start_ring(self, low=0, high=4):
+            for way, sub in arrivals(0)[low:high]:
                 self.ring(way, 0, sub).start()
 
-        def start(self):
-            self.start_ring()
+        def start(self, high=4):
+            self.start_ring(0, high)
             for sub in range(2):
                 self.mate(pos, 0, sub).start()
 
@@ -353,9 +363,9 @@
     class Across(Gather):
         def __init__(self, l):
             self.l, self.to = l, {"fsdp": middle}
-            self.a = Gather(spare(l), layers + l - split, by_z)
-            self.b = Gather(spare(l), layers + l - split, by_ring)
-            self.out = Gather(l, layers + l - split, by_ring)
+            self.a = Gather(spare(l), layers + l - split, by_z(l))
+            self.b = Gather(spare(l), layers + l - split, by_ring(l))
+            self.out = Gather(l, layers + l - split, by_ring(l))
 
         def sems(self, slot, sub):
             at = (self.l - split, slot, sub)
@@ -363,7 +373,7 @@
 
         def first(self, sub):
             pair = self.sems(ring + 1, sub)
-            return send_rows(self.to, self.l, spare(self.l), pos, sub, by_z, *pair)
+            return send_rows(self.to, self.l, spare(self.l), pos, sub, by_z(self.l), *pair)
 
         def open_first(self):
             for sub in range(2):
@@ -375,7 +385,7 @@
 
         def relay(self, owner, slot, sub):
             pair = self.sems(slot, sub)
-            return send_rows(self.to, self.l, spare(self.l), owner, sub, by_ring, *pair)
+            return send_rows(self.to, self.l, spare(self.l), owner, sub, by_ring(self.l), *pair)
 
         def mate_b(self, owner, slot, sub):
             at = (self.l - split, slot, sub)
@@ -385,7 +395,7 @@
                 spare(self.l),
                 owner,
                 sub,
-                by_ring,
+                by_ring(self.l),
                 r["again_send"].at[at],
                 r["again_recv"].at[at],
             )
@@ -429,12 +439,17 @@
             both = jnp.logical_and(both, inner)
         return both
 
-    def give_mixed(c):
+    cut = first_cols(last)
+    spans = ((0, cut), (cut, cols - cut))
+
+    def give_mixed(c, which):
+        low, wide = spans[which]
+        at = pl.ds(pl.multiple_of(end * cols + low, 128), wide)
         return pltpu.make_async_remote_copy(
-            src_ref=r["b"].at[1, rows_of(c), cols_of(end)],
-            dst_ref=r["mixed"].at[rows_of(c)],
-            send_sem=r["mixed_send"].at[c],
-            recv_sem=r["mixed_recv"].at[c],
+            src_ref=r["b"].at[1, rows_of(c), at],
+            dst_ref=r["mixed"].at[rows_of(c), pl.ds(low, wide)],
+            send_sem=r["mixed_send"].at[which, c],
+            recv_sem=r["mixed_recv"].at[which, c],
             device_id={"fsdp": jnp.where(inner, end, middle)},
             device_id_type=MESH,
         )
@@ -453,10 +468,10 @@
         pl.semaphore_signal(barrier, inc=1, device_id=peer, device_id_type=MESH)
     pl.semaphore_wait(barrier, len(peers))
 
+    opening = gathers[0]
+    opening.step(0, opening.mate, lambda way: take_near(way).wait())
     for l in range(layers):
         take_own(l).wait()
-    opening = gathers[0]
-    opening.step(0, opening.mate, lambda way: take_near(way).wait())
     for half_block in range(2):
         opening.mate(pos, 0, half_block).start()
     gathers[1].start()
@@ -467,16 +482,18 @@
 
     take_tokens.wait()
 
-    def init_body(t, carry):
+    def init_body(way, t, carry):
         at = pl.ds(pl.multiple_of(t * tile, tile), tile)
-        code = jnp.dot(r["hot"][...], r["table"][:, at], preferred_element_type=jnp.float32)
+        code = jnp.dot(r["hot"][way], r["table"][:, at], preferred_element_type=jnp.float32)
+        at = pl.ds(pl.multiple_of(way * (width // 2) + t * tile, tile), tile)
         slot = lax.broadcasted_iota(jnp.int32, code.shape, 0)
         value = r["b"][1, :, at].astype(jnp.float32) + code
         r["stream"][:, at] = jnp.where(slot < count, value, 0.0)
         return carry
 
     with jax.named_scope("init"):
-        lax.fori_loop(0, width // tile, init_body, 0)
+        for way in range(2):
+            lax.fori_loop(0, width // 2 // tile, functools.partial(init_body, way), 0)
     with jax.named_scope("opening"):
         for hop in range(1, half - 1):
             opening.step(hop, opening.mate)
@@ -489,7 +506,7 @@
             centre = jnp.sum(x, axis=1, keepdims=True) * (1.0 / width)
             shifted = x - centre
             spread = jnp.sum(shifted * shifted, axis=1, keepdims=True) * (1.0 / width)
-            normed = shifted * lax.rsqrt(spread + norm_eps) * r["gain"][l]
+            normed = shifted * lax.rsqrt(spread + norm_eps) * r["gain"][l : l + 1]
             r["x"][at] = normed.astype(jnp.bfloat16)
             return carry
 
@@ -538,14 +555,23 @@
     def branch(l, slot, c, owner):
         multiply(slot, rows_of(c), branch_into(l, c, owner))
 
-    def result(slot, at_rows, start, owner, put):
-        def take(t, at, out):
-            mine = pl.ds(pl.multiple_of(owner * cols + t * tile, tile), tile)
+    def result(slot, at_rows, start, owner, put, which=None):
+        def take(low, at, out):
+            mine = pl.ds(pl.multiple_of(owner * cols + low, 128), out.shape[1])
             place_of = start + lax.broadcasted_iota(jnp.int32, out.shape, 0)
             total = r["stream"][at_rows, mine] + out.astype(jnp.float32)
             put(mine, at, jnp.where(place_of < count, total, 0.0).astype(jnp.bfloat16))
 
-        multiply(slot, at_rows, take)
+        if which is None:
+            multiply(slot, at_rows, lambda t, at, out: take(t * tile, at, out))
+            return
+        low, wide = spans[which]
+        for begin in range(low, low + wide, tile):
+            at = pl.ds(begin, min(tile, low + wide - begin))
+            out = jnp.dot(
+                r["x"][at_rows], r["w"][slot, :, at], preferred_element_type=jnp.float32
+            )
+            take(begin, at, out.astype(jnp.bfloat16))
 
     def over_chunks(body, low=0, high=chunks):
         lax.fori_loop(low, high, lambda c, carry: (body(c), carry)[1], 0)
@@ -621,14 +647,18 @@
             sent_pieces(1)
         with jax.named_scope("outer_feeds"):
             across[last].open_first()
+            for half_block in both_halves:
+                across[last].first(half_block).wait_send()
             across[last].relay_own()
             across[last].out.mid(across[last].relay)
             across[last].out.finish(across[last].relay)
         with jax.named_scope("outer_mixed"):
-            over_chunks(lambda c: give_mixed(c).wait_recv())
+            for which in range(2):
+                over_chunks(lambda c: give_mixed(c, which).wait_recv())
         for l in range(split, layers):
-            for half_block in both_halves:
-                across[l].first(half_block).wait_send()
+            if l < last:
+                for half_block in both_halves:
+                    across[l].first(half_block).wait_send()
             across[l].out.sent_ring()
             for owner, slot, half_block in across[l].out.blocks():
                 across[l].relay(owner, slot, half_block).wait_send()
@@ -649,6 +679,9 @@
 
     def wait_spare(l):
         across[l].a.wait_mates()
+        wait_again(l)
+
+    def wait_again(l):
         for owner, slot, half_block in across[l].b.blocks():
             across[l].mate_b(owner, slot, half_block).wait_recv()
 
@@ -661,31 +694,34 @@
         with jax.named_scope("forward_0b"):
             forward(0, 0, chunks - 1, chunks)
         with jax.named_scope("forward_1"):
-            forward(0, 1, 0, chunks // 2)
+            forward(0, 1, 0, 1)
         gathers[split].start()
+        with jax.named_scope("forward_1b"):
+            forward(0, 1, 1, chunks - 1)
         open_spare(split)
-        with jax.named_scope("forward_1b"):
-            forward(0, 1, chunks // 2, chunks)
+        with jax.named_scope("gather_1_finish"):
+            gathers[1].finish()
+        with jax.named_scope("forward_1c"):
+            forward(0, 1, chunks - 1, chunks)
         with jax.named_scope("gather_1_end"):
-            gathers[1].end()
+            gathers[1].wait_mates()
         with jax.named_scope("layer_1"):
             over_chunks(layer_one)
         with jax.named_scope("gather_2_mid"):
             gathers[split].mid()
-            across[split].a.mid()
         with jax.named_scope("forward_2"):
             forward(1, 0, 0, chunks // 2)
+        with jax.named_scope("spare_mid"):
+            across[split].a.mid()
         with jax.named_scope("spare_relay"):
             relay_spare(split)
         with jax.named_scope("forward_2b"):
             forward(1, 0, chunks // 2, chunks)
-        gathers[last].start()
         with jax.named_scope("gather_2_end"):
             gathers[split].finish()
             across[split].a.finish()
-        with jax.named_scope("spare_open"):
-            open_spare(last)
-        with jax.named_scope("wait_mates"):
+        gathers[last].start(2)
+        with jax.named_scope("mates_2"):
             gathers[split].wait_mates()
             wait_spare(split)
 
@@ -699,41 +735,71 @@
             send_piece(split, 1, c)
 
         with jax.named_scope("layer_2"):
-            over_chunks(body)
-        with jax.named_scope("last_mid"):
+            over_chunks(body, 0, 1)
+        with jax.named_scope("spare_open"):
+            open_spare(last)
+        with jax.named_scope("layer_2b"):
+            over_chunks(body, 1, chunks - 1)
+        gathers[last].start_ring(2, 4)
+        with jax.named_scope("layer_2c"):
+            over_chunks(body, chunks - 1, chunks)
+        with jax.named_scope("last_spare_mid"):
             across[last].a.mid()
-            gathers[last].mid()
-        with jax.named_scope("last_relay"):
-            relay_spare(last)
-        with jax.named_scope("last_spare"):
-            across[last].a.finish()
-            wait_spare(last)
             sent_pieces(1)
 
-        def put_away(c):
-            def put(mine, at, value):
-                r["b"][1, rows_of(c), mine] = value
-
-            return put
-
-        def put_here(mine, at, value):
-            r["mixed"][:, at] = value
-
-        def body(c):
+        def prepare(c):
             wait_pieces(last - 1, 0, c)
             wait_pieces(last - 1, 1, c)
             add_chunk(last, c)
             norm_chunk(last, c)
-            result(spare(last), rows_of(c), c * part, end, put_away(c))
-            give_mixed(c).start()
-
-        with jax.named_scope("layer_3"):
-            over_chunks(body)
+
+        with jax.named_scope("last_norm"):
+            over_chunks(prepare, 0, chunks // 2)
+        with jax.named_scope("last_mid"):
+            gathers[last].mid()
+        with jax.named_scope("last_spare"):
+            across[last].a.finish()
+        with jax.named_scope("last_mates"):
+            across[last].a.wait_mates()
+
+        def put_away(c):
+            def put(mine, at, value):
+                r["b"][1, rows_of(c), mine] = value
+
+            return put
+
+        def put_here(mine, at, value):
+            r["mixed"][:, at] = value
+
+        def end_result(which):
+            def body(c):
+                result(spare(last), rows_of(c), c * part, end, put_away(c), which)
+                give_mixed(c, which).start()
+
+            return body
+
+        with jax.named_scope("layer_3_a"):
+            over_chunks(end_result(0), 0, chunks // 2)
+
+        def rest(c):
+            prepare(c)
+            end_result(0)(c)
+            end_result(1)(c)
+
+        with jax.named_scope("last_relay"):
+            relay_spare(last)
+            gathers[last].finish()
+            wait_again(last)
+        with jax.named_scope("layer_3_b"):
+            over_chunks(end_result(1), 0, chunks // 2)
+        with jax.named_scope("layer_3_c"):
+            over_chunks(rest, chunks // 2, chunks)
         with jax.named_scope("last_gather_end"):
-            gathers[last].end()
+            gathers[last].wait_mates()
         with jax.named_scope("layer_3_own"):
             result(last, pl.ds(0, tok), 0, place, put_here)
-        sent_pieces(last - 1)
+        with jax.named_scope("all_sent"):
+            sent_pieces(last - 1)
         for l in range(split, layers):
             gathers[l].sent_ring()
             gathers[l].sent_mates()
@@ -741,7 +807,9 @@
             across[l].a.sent_mates()
             for owner, slot, half_block in across[l].b.blocks():
                 across[l].mate_b(owner, slot, half_block).wait_send()
-        over_chunks(lambda c: give_mixed(c).wait_send())
+        with jax.named_scope("mixed_sent"):
+            for which in range(2):
+                over_chunks(lambda c: give_mixed(c, which).wait_send())
 
     gathers[1].sent_ring()
     gathers[1].sent_mates()
@@ -774,8 +842,8 @@
         "again_recv": dma((2, 1 + 2 * half, 2)),
         "send": dma((layers - 1, 2, n - 1, chunks)),
         "recv": dma((layers - 1, 2, n - 1, chunks)),
-        "mixed_send": dma((chunks,)),
-        "mixed_recv": dma((chunks,)),
+        "mixed_send": dma((2, chunks)),
+        "mixed_recv": dma((2, chunks)),
         "free": pltpu.SemaphoreType.REGULAR,
     }
     return pl.pallas_call(
@@ -788,7 +856,7 @@
             collective_id=1, has_side_effects=True, vmem_limit_bytes=67043328
         ),
         name="layers",
-    )(own, from_last, from_next, tokens, hot, table, gain[:, None, :], counts)
+    )(own, from_last, from_next, tokens, hot, table, gain, counts)
 
 
 def ring_pairs(n_dp):
@@ -810,16 +878,12 @@
     middle = lax.reduce_precision(exact - high, 8, 7)
     low = exact - high - middle
     lane = jnp.zeros((GRID, 2 * quarter), jnp.float32)
-    rows = jnp.concatenate([high, middle, low, lane], axis=0).astype(jnp.bfloat16)
-    empty = jnp.zeros_like(rows)
-    return jnp.concatenate(
-        [jnp.concatenate([rows, empty], axis=1), jnp.concatenate([empty, rows], axis=1)], axis=0
-    )
+    return jnp.concatenate([high, middle, low, lane], axis=0).astype(jnp.bfloat16)
 
 
 def one_hot(patch_index):
-    lane = lax.broadcasted_iota(jnp.int32, (1, 8 * GRID), 1)
-    which = jnp.where(lane < 4 * GRID, patch_index[:, None] // GRID, patch_index[:, None] % GRID)
+    lane = lax.broadcasted_iota(jnp.int32, (1, 1, 4 * GRID), 2)
+    which = jnp.stack([patch_index // GRID, patch_index % GRID])[:, :, None]
     return (lane % GRID == which).astype(jnp.bfloat16)
 
 

time: 249 us -> 235 us (0.944)
  Pallas kernels: 240 us -> 226 us
    pallas_call x1, Pallas kernels: 193 us -> 185 us  [run_layers(): pl.pallas_call(functools.partial(layers_kernel, n_dp, n, chunks, names +...]
    pallas_call x1, Pallas kernels: 29.1 us -> 23.9 us  [adam_all(): pl.pallas_call(adam_kernel, grid=(layers, rows // part), out_shape=[f32,...]
  transfers between devices with their start and end apart: 2 -> 2, of which waited for: 0 -> 0; matrix products, arithmetic and copies ran while one was open for 1% -> 1% of each run, Pallas kernels for 12% -> 10%
where the time goes in v3:
time: 235 us
  Pallas kernels  226 us (96%)
  local copies, waits for them, and re-layouts  2.35 us (1%)
    pallas_call x1, Pallas kernels, run_layers(): pl.pallas_call(functools.partial(layers_kernel, n_dp, n, chunks, names +...  185 us
    pallas_call x1, Pallas kernels, adam_all(): pl.pallas_call(adam_kernel, grid=(layers, rows // part), out_shape=[f32,...  23.9 us
    pallas_call x1, Pallas kernels, total_over_mesh(): pl.pallas_call(functools.partial(total_kernel, sizes, chunks), out_shape=...  17.5 us
  transfers between devices with their start and end apart: 2, of which 0 were waited for; matrix products, arithmetic and copies ran while one was open for 1% of the time, Pallas kernels for 10%

profile of v3, /device:TPU:0, one launch (start us, length us, event | category | flops | bytes accessed | tf_op | source)
XLA Modules:
  0.0 234.9 jit_solution(11919788245399184674)
XLA Ops:
  1.3 0.0 copy-start
  1.3 17.5 %total.1 = (f32[8,128]{1,0:T(8,128)}, bf16[512,1024]{1,0:T(8,128)(2,1)}) custom-call(f32[1]{0:T(128)} %bitcast.3.clip_ref, f32[4,512,1024]{2,1,0:T(8,128)} %g_ref.3, f32[4,512,1024]{2,1,0:T(8,128)} %p_ref.3, f32[4,512,1024]{2,1,0:T(8,128)} %m_ref.3, f32[4,512,1024]{2,1,0:T(8,128)} %s_ref.3), custom_call_target="tpu_custom_call" | custom-call | tf_op jit(solution)/shard_map/total/pallas_call | solution.py:135
  18.8 0.7 collective-permute-start
  19.5 1.4 collective-permute-start.1
  20.9 0.0 copy-done
  20.9 0.2 fusion.2
  21.9 0.1 pad.3.clone
  21.9 23.9 %adam.1 = (f32[4,512,1024]{2,1,0:T(8,128)}, f32[4,512,1024]{2,1,0:T(8,128)}, f32[4,512,1024]{2,1,0:T(8,128)}, bf16[4,512,1024]{2,1,0:T(8,128)(2,1)}) custom-call(f32[8,128]{1,0:T(8,128)} %get-tuple-element.10.f_ref, f32[4,512,1024]{2,1,0:T(8,128)} %p_ref.3, f32[4,512,1024]{2,1,0:T(8,128)} %m_ref.3, f32[4,512,1024]{2,1,0:T(8,128)} %s_ref.3, f32[4,512,1024]{2,1,0:T(8,128)} %g_ref.3), custom_call_target="tpu_custom_call" | custom-call | flops 41943040 | bytes 62914560 | tf_op jit(solution)/shard_map/adam/pallas_call | solution.py:174
  45.9 0.9 compare_convert_fusion.refs_4_
  46.8 0.8 maximum_maximum_fusion.refs_5_
  47.6 0.0 collective-permute-done.refs_1_
  47.6 0.0 collective-permute-done.1.refs_2_
  47.6 185.0 %layers.1 = bf16[512,1024]{1,0:T(8,128)(2,1)} custom-call(bf16[4,512,1024]{2,1,0:T(8,128)(2,1)} %get-tuple-element.14.refs_0_, bf16[512,1024]{1,0:T(8,128)(2,1)} %collective-permute-done.refs_1_, bf16[512,1024]{1,0:T(8,128)(2,1)} %collective-permute-done.1.refs_2_, bf16[512,4096]{1,0:T(8,128)(2,1)} %refs_3_.1, ...), custom_call_target="tpu_custom_call" | custom-call | tf_op jit(solution)/shard_map/layers/pallas_call | solution.py:849
  232.6 2.3 copy.16
  (6 shorter events, 0.1 us)
Async XLA Ops:
  1.3 19.7 %copy-start = (s32[512]{0:T(512)S(1)}, s32[512]{0:T(512)}, u32[]{:S(2)}) copy-start(s32[512]{0:T(512)} %param.11) | copy-start | bytes 6148
  18.8 28.8 %collective-permute-start = (bf16[512,1024]{1,0:T(8,128)(2,1)}, bf16[512,1024]{1,0:T(8,128)(2,1)}, u32[]{:S(2)}, u32[]{:S(2)}) collective-permute-start(bf16[512,1024]{1,0:T(8,128)(2,1)} %get-tuple-element.15), channel_id=1, source_target_pairs={{0,8},{4,12},{8,24},{12,28},{24,16},{28,20},{16,0},{20,4},{1,9},{5... | collective-permute-start | bytes 3145736 | tf_op jit(solution)/shard_map/ppermute | solution.py:904
  19.5 28.1 %collective-permute-start.1 = (bf16[512,1024]{1,0:T(8,128)(2,1)}, bf16[512,1024]{1,0:T(8,128)(2,1)}, u32[]{:S(2)}, u32[]{:S(2)}) collective-permute-start(bf16[512,1024]{1,0:T(8,128)(2,1)} %get-tuple-element.15), channel_id=1, source_target_pairs={{8,0},{12,4},{24,8},{28,12},{16,24},{20,28},{0,16},{4,20},{9,1},{1... | collective-permute-start | bytes 3145736 | tf_op jit(solution)/shard_map/ppermute | solution.py:905
